TPU v7x, 32 devices: a whole 2x2x4 slice. The times are simulated.
32 devices in a mesh: tp: 4 (over z), dp: 8 (over y, x, core).
Axes of the slice: x: 2, y: 2, z: 4, core: 2. Of those that a mesh axis runs over, the one named last changes fastest.
Arguments:
- w_query: bfloat16 [16, 1024, 1024], P(None, ('dp', 'tp'))
- w_key: bfloat16 [16, 1024, 1024], P(None, ('dp', 'tp'))
- w_value: bfloat16 [16, 1024, 1024], P(None, ('dp', 'tp'))
- w_out: bfloat16 [16, 1024, 1024], P(None, ('dp', 'tp'))
- w_gate: bfloat16 [16, 1024, 2816], P(None, ('dp', 'tp'))
- w_up: bfloat16 [16, 1024, 2816], P(None, ('dp', 'tp'))
- w_down: bfloat16 [16, 2816, 1024], P(None, ('dp', 'tp'))
- w_head: bfloat16 [1024, 151936], P(('dp', 'tp'))
Outputs:
- output 1: bfloat16 [16, 3072, 1024], P(None, 'tp')
- output 2: bfloat16 [16, 1024, 1024], P(None, None, 'tp')
- output 3: bfloat16 [16, 5632, 1024], P(None, 'tp')
- output 4: bfloat16 [16, 1024, 2816], P(None, None, 'tp')
- output 5: bfloat16 [151936, 1024], P('tp')
All inputs are finite; a program needn't handle non-finite values.
Results may differ from a plain program's by a relative error of at most 0.001.
Values are sent between devices in bfloat16 or wider.
A program may use at most 1 GiB of HBM per device.

v0:
```python
import functools

import jax
import jax.numpy as jnp
from jax import lax
from jax.experimental import pallas as pl
from jax.experimental.pallas import tpu as pltpu
from jax.sharding import PartitionSpec as P


MESH = pl.DeviceIdType.MESH
LANES = 128
VMEM = 67_000_000
AHEAD = 4
BUFFERS = 6
LAG = 2
SHARE_AT = 14
GROUP = 2


class Plan:
    def __init__(self, tp, dp, w_query, w_gate, w_out, w_down, w_head):
        self.tp, self.dp = tp, dp
        self.layers, self.rows, columns = w_query.shape
        self.part = columns // tp
        self.wide = w_gate.shape[2] // tp
        self.vocab = w_head.shape[1] // tp
        self.head_tiles = w_head.shape[1] // LANES
        self.chunk = 3 * self.part + 2 * self.wide
        self.wide_window = -(-self.wide // LANES) * LANES
        self.layer_window = 3 * self.part + 2 * self.wide_window
        self.head_chunks = -(-self.vocab // self.chunk)
        self.tail = self.vocab - (self.head_chunks - 1) * self.chunk
        self.chunks = self.layers + self.head_chunks
        self.tail_window = -(-(self.tail + LANES) // LANES) * LANES
        self.window_tiles = (self.head_chunks - 1) * self.chunk // LANES + self.tail_window // LANES
        self.out_rows, self.down_rows = w_out.shape[1], w_down.shape[1]
        self.share = self.layers // dp

    def wide_base(self, rank):
        return (self.wide * rank) // LANES

    def head_base(self, rank):
        base = (self.vocab * rank) // LANES
        return base - (rank // (self.tp - 1)) * (self.vocab * (self.tp - 1) // LANES + self.window_tiles - self.head_tiles)


def gather_kernel(plan, q, k, v, o, g, u, d, h, slabs, own_0, own_1, stop_0, stop_1, zbuf, tbuf, z_recv, z_send,
                  local, x_recv, y_recv, a_recv, b_recv, pair_recv, send, stop_recv, share_recv, share_send):
    z, dp = lax.axis_index("tp"), lax.axis_index("dp")
    core, x, y = dp % 2, (dp // 2) % 2, dp // 4
    x_peer = y * 4 + (1 - x) * 2 + core
    y_peer = (1 - y) * 4 + x * 2 + core
    diagonal = (1 - y) * 4 + (1 - x) * 2 + core
    pair = dp + 1 - 2 * core
    rows, chunk, tail = plan.rows, plan.chunk, plan.tail
    layers, last = plan.layers, plan.chunks - 1
    my_rows = pl.ds(pl.multiple_of(z * rows, rows), rows)

    def lanes(first_tile, width):
        return pl.ds(pl.multiple_of(first_tile * LANES, LANES), width)

    def remote(source, target, send_sem, recv_sem, **to):
        pltpu.make_async_remote_copy(source, target, send_sem, recv_sem, device_id=to, device_id_type=MESH).start()

    def wait_for(ref, sem):
        pltpu.make_async_copy(ref, ref, sem).wait()


    def exchange(pieces, chunks, index):
        for step in range(1, plan.tp):
            rank = (z + step + core * (plan.tp - 2 * step)) % plan.tp
            for source, column, width in pieces(rank):
                target = zbuf.at[chunks, my_rows, pl.ds(column, width)]
                remote(source, target, z_send.at[index], z_recv.at[index], tp=rank)
        for source, column, width in pieces(z):
            target = zbuf.at[chunks, my_rows, pl.ds(column, width)]
            pltpu.make_async_copy(source, target, z_recv.at[index]).start()

    def layer_pieces(some):
        def pieces(rank):
            part, wide = plan.part, plan.wide_window
            narrow = lanes(rank * (part // LANES), part)
            window = lanes(plan.wide_base(rank), wide)
            return [
                (q.at[some, :, narrow], 0, part),
                (k.at[some, :, narrow], part, part),
                (v.at[some, :, narrow], 2 * part, part),
                (g.at[some, :, window], 3 * part, wide),
                (u.at[some, :, window], 3 * part + wide, wide),
            ]

        return pieces

    def head_pieces(step, width):
        def pieces(rank):
            return [(h.at[:, lanes(plan.head_base(rank) + step * (chunk // LANES), width)], 0, width)]

        return pieces

    def start_exchange(index):
        @pl.when((index < layers) & (index % GROUP == 0))
        def _():
            some = pl.ds(index, GROUP)
            exchange(layer_pieces(some), some, index)

        @pl.when((index >= layers) & (index < last))
        def _():
            exchange(head_pieces(index - layers, chunk), index, index)

        @pl.when(index == last)
        def _():
            exchange(head_pieces(last - layers, plan.tail_window), last, last)

    def wait_exchange(index, width):
        wait_for(zbuf.at[index, :, pl.ds(0, width)], z_recv.at[index])


    def turn(slot, tile, index, source_tile):
        tbuf[slot, pl.ds(tile * LANES, LANES), :] = zbuf[index, :, pl.ds(source_tile * LANES, LANES)].T

    def store(slot, first, index, to, count):
        pltpu.make_async_copy(
            tbuf.at[slot, pl.ds(first, count), :], slabs.at[dp, index, pl.ds(to, count), :], local.at[slot]
        ).start()

    def make_layer(index, slot):
        @pl.when(index % GROUP == 0)
        def _():
            wait_for(zbuf.at[pl.ds(index, GROUP), :, pl.ds(0, plan.layer_window)], z_recv.at[index])

        for tile in range(plan.layer_window // LANES):
            turn(slot, tile, index, tile)
        shift = plan.wide * z - plan.wide_base(z) * LANES
        narrow, wide, window = 3 * plan.part, plan.wide, plan.wide_window
        store(slot, 0, index, 0, narrow)
        store(slot, pl.multiple_of(narrow + shift, 16), index, narrow, wide)
        store(slot, pl.multiple_of(narrow + window + shift, 16), index, narrow + wide, wide)

    head_shift = plan.vocab * z - plan.head_base(z) * LANES

    def make_head(index, slot):
        @pl.when(index == layers)
        def _():
            wait_exchange(index, chunk)

        @pl.when(index < last - 1)
        def _():
            wait_exchange(index + 1, chunk)

        @pl.when(index == last - 1)
        def _():
            wait_exchange(last, plan.tail_window)

        tiles = chunk // LANES
        for tile in range(tiles):
            turn(slot, tile, index, tile)
        for tile in range(2):
            turn(slot, tiles + tile, index + 1, tile)
        store(slot, pl.multiple_of(head_shift, 16), index, 0, chunk)

    def make_tail(slot):
        for tile in range(plan.tail_window // LANES):
            turn(slot, tile, last, tile)
        store(slot, pl.multiple_of(head_shift, 16), last, 0, tail)


    def slab_view(index):
        return lambda owner, first, count: slabs.at[owner, index, pl.ds(first, count), :]

    def push(part, index, recv, to):
        remote(part, part, send.at[index], recv.at[index], dp=to)

    def send_own(view, index, slot, count):
        own = view(dp, 0, count)
        wait_for(own, local.at[slot])
        push(own, index, x_recv, x_peer)
        push(own, index, y_recv, y_peer)
        push(own, index, pair_recv, pair)

    def forward(view, index, count):
        half = count // 2
        wait_for(view(x_peer, 0, count), x_recv.at[index])
        push(view(x_peer, half, half), index, b_recv, y_peer)
        push(view(x_peer, 0, count), index, pair_recv, pair)
        wait_for(view(y_peer, 0, count), y_recv.at[index])
        push(view(y_peer, 0, half), index, a_recv, x_peer)
        push(view(y_peer, 0, count), index, pair_recv, pair)

    def forward_diagonal(view, index, count):
        half = count // 2
        wait_for(view(diagonal, 0, half), a_recv.at[index])
        wait_for(view(diagonal, half, half), b_recv.at[index])
        push(view(diagonal, 0, count), index, pair_recv, pair)

    def finish(view, index, count):
        wait_for(view(pl.ds(0, 7), 0, count), send.at[index])
        wait_for(view(pl.ds(0, 4), 0, count), pair_recv.at[index])

    def finish_exchange(index, window):
        wait_for(zbuf.at[index, pl.ds(0, (plan.tp - 1) * rows), pl.ds(0, window)], z_send.at[index])


    def pieces(source_dp, to, place):
        all_rows = plan.tp * 2 * plan.down_rows
        downs = pl.ds(pl.multiple_of(place * plan.down_rows, 8), plan.down_rows)
        outs = pl.ds(pl.multiple_of(all_rows + place * plan.out_rows, 8), plan.out_rows)
        stop_downs, stop_outs = pl.ds(0, plan.down_rows), pl.ds(plan.down_rows, plan.out_rows)
        found = []
        for n, (stop, own) in enumerate(((stop_0, own_0), (stop_1, own_1))):
            layer = to * 2 + n
            found.append((d.at[layer], stop.at[source_dp, stop_downs, :], own.at[downs, :], n))
            found.append((o.at[layer], stop.at[source_dp, stop_outs, :], own.at[outs, :], n))
        return found

    my_rank = dp // 2
    my_place = (dp % 2) * plan.tp + z
    stays = my_rank == z

    def share_in_plane():
        for step in range(1, plan.dp):
            to = (dp + step) % plan.dp

            @pl.when(stays)
            def _(to=to):
                for part, _, final, n in pieces(dp, to, my_place):
                    remote(part, final, share_send.at[n], share_recv.at[n], dp=to)

            @pl.when(jnp.logical_not(stays))
            def _(to=to):
                for part, stop, _, n in pieces(dp, to, my_place):
                    remote(part, stop, share_send.at[n], stop_recv.at[n, dp], dp=to)

        @pl.when(stays)
        def _():
            for part, _, final, n in pieces(dp, dp, my_place):
                pltpu.make_async_copy(part, final, share_recv.at[n]).start()

    def share_to_rank(source_dp):
        rank, place = source_dp // 2, (source_dp % 2) * plan.tp + z

        @pl.when((rank != z) & (source_dp == dp))
        def _():
            for part, _, final, n in pieces(dp, dp, place):
                remote(part, final, share_send.at[n], share_recv.at[n], tp=rank)

        @pl.when((rank != z) & (source_dp != dp))
        def _():
            for n, stop in enumerate((stop_0, stop_1)):
                wait_for(stop.at[source_dp], stop_recv.at[n, source_dp])
            for _, stop, final, n in pieces(source_dp, dp, place):
                remote(stop, final, share_send.at[n], share_recv.at[n], tp=rank)

    start_exchange(0)
    share_in_plane()
    for index in range(GROUP, AHEAD):
        start_exchange(index)

    def step(index, _):
        slot = index % 2

        @pl.when(index + AHEAD < plan.chunks)
        def _():
            start_exchange(index + AHEAD)

        @pl.when((index >= SHARE_AT) & (index < SHARE_AT + 2 * plan.dp) & (index % 2 == SHARE_AT % 2))
        def _():
            share_to_rank((index - SHARE_AT) // 2)

        @pl.when(index < layers)
        def _():
            make_layer(index, slot)

        @pl.when(index >= layers)
        def _():
            make_head(index, slot)

        send_own(slab_view(index), index, slot, chunk)

        @pl.when(index >= LAG)
        def _():
            forward(slab_view(index - LAG), index - LAG, chunk)

        @pl.when(index >= 2 * LAG)
        def _():
            forward_diagonal(slab_view(index - 2 * LAG), index - 2 * LAG, chunk)

        return 0

    lax.fori_loop(0, last, step, 0)

    make_tail(last % 2)
    send_own(slab_view(last), last, last % 2, tail)
    for index in range(last - LAG, last):
        forward(slab_view(index), index, chunk)
    forward(slab_view(last), last, tail)
    for index in range(last - 2 * LAG, last):
        forward_diagonal(slab_view(index), index, chunk)
    forward_diagonal(slab_view(last), last, tail)

    def drain(index, _):
        finish(slab_view(index), index, chunk)

        @pl.when((index < layers) & (index % GROUP == 0))
        def _():
            sent = pl.ds(0, (plan.tp - 1) * rows)
            wait_for(zbuf.at[pl.ds(index, GROUP), sent, pl.ds(0, plan.layer_window)], z_send.at[index])

        @pl.when(index >= layers)
        def _():
            finish_exchange(index, chunk)

        return 0

    lax.fori_loop(0, last, drain, 0)
    finish(slab_view(last), last, tail)
    finish_exchange(last, plan.tail_window)
    for n, own in enumerate((own_0, own_1)):
        wait_for(own, share_recv.at[n])
        for parts in (8, 5):
            wait_for(own.at[pl.ds(0, parts * (plan.down_rows + plan.out_rows)), :], share_send.at[n])


def gather(plan, *args):
    dma = pltpu.SemaphoreType.DMA
    per_chunk = dma((plan.chunks,))
    columns = args[3].shape[2]
    share_rows = plan.down_rows + plan.out_rows
    hbm = pl.BlockSpec(memory_space=pltpu.HBM)
    shapes = [(plan.dp, plan.chunks, plan.chunk, LANES)]
    shapes += [(plan.tp * 2 * share_rows, columns)] * 2 + [(plan.dp, share_rows, columns)] * 2
    return pl.pallas_call(
        functools.partial(gather_kernel, plan),
        out_shape=[jax.ShapeDtypeStruct(shape, jnp.bfloat16) for shape in shapes],
        in_specs=[hbm] * 8,
        out_specs=[hbm] * len(shapes),
        scratch_shapes=[
            pltpu.VMEM((plan.chunks, plan.tp * plan.rows, plan.layer_window), jnp.bfloat16),
            pltpu.VMEM((2, plan.chunk + 2 * LANES, LANES), jnp.bfloat16),
            per_chunk, per_chunk, dma((2,)),
            per_chunk, per_chunk, per_chunk, per_chunk, per_chunk, per_chunk,
            dma((2, plan.dp)), dma((2,)), dma((2,)),
        ],
        compiler_params=pltpu.CompilerParams(has_side_effects=True),
        name="gather",
    )(*args)[:3]


def place_slabs(plan, slabs, first, count, shapes, store, held=()):
    hbm = pl.BlockSpec(memory_space=pltpu.HBM)
    depth = min(BUFFERS, count)
    ahead = depth // 2

    def body(slab, *refs):
        outs, (buffers, loads, stores) = refs[len(held):-3], refs[-3:]

        def each_size(chunk, act):
            if first + count == plan.chunks:
                pl.when(chunk < plan.chunks - 1)(lambda: act(plan.chunk))
                pl.when(chunk == plan.chunks - 1)(lambda: act(plan.tail))
            else:
                act(plan.chunk)

        def load(i, rows):
            for owner in range(plan.dp):
                pltpu.make_async_copy(
                    slab.at[owner, first + i, pl.ds(0, rows), :],
                    buffers.at[i % depth, pl.ds(0, rows), pl.ds(owner * LANES, LANES)],
                    loads.at[i % depth],
                ).start()

        def wait(i, rows, sem):
            buffer = buffers.at[i % depth, pl.ds(0, rows), :]
            pltpu.make_async_copy(buffer, buffer, sem.at[i % depth]).wait()

        def write(i, rows):
            wait(i, rows, loads)
            for source, target in store(buffers.at[i % depth], first + i, rows, outs):
                pltpu.make_async_copy(source, target, stores.at[i % depth]).start()

        def step(i, _):
            @pl.when(i >= depth)
            def _():
                each_size(first + i - depth, lambda rows: wait(i - depth, rows, stores))

            @pl.when(i < count)
            def _():
                each_size(first + i, lambda rows: load(i, rows))

            @pl.when((i >= ahead) & (i < count + ahead))
            def _():
                each_size(first + i - ahead, lambda rows: write(i - ahead, rows))

            return 0

        lax.fori_loop(0, count + depth, step, 0)

    outs = [jax.ShapeDtypeStruct(shape, jnp.bfloat16) for shape in shapes]
    return pl.pallas_call(
        body,
        in_specs=[hbm] * (1 + len(held)),
        out_specs=[hbm] * len(outs),
        out_shape=outs,
        scratch_shapes=[
            pltpu.VMEM((depth, plan.chunk, plan.dp * LANES), jnp.bfloat16),
            pltpu.SemaphoreType.DMA((depth,)),
            pltpu.SemaphoreType.DMA((depth,)),
        ],
        input_output_aliases={1 + n: n for n in range(len(held))},
        cost_estimate=pl.CostEstimate(
            flops=10**7, bytes_accessed=4 * count * plan.chunk * plan.dp * LANES, transcendentals=0
        ),
        compiler_params=pltpu.CompilerParams(vmem_limit_bytes=VMEM),
    )(slabs, *held)


def place_layers(plan, slabs):
    narrow, wide, width = 3 * plan.part, 2 * plan.wide, plan.dp * LANES

    def store(buffer, chunk, rows, outs):
        return [
            (buffer.at[pl.ds(0, narrow), :], outs[0].at[chunk]),
            (buffer.at[pl.ds(narrow, wide), :], outs[1].at[chunk]),
        ]

    shapes = [(plan.layers, narrow, width), (plan.layers, wide, width)]
    return place_slabs(plan, slabs, 0, plan.layers, shapes, store)


def place_head(plan, slabs, first, count, *held):
    def store(buffer, chunk, rows, outs):
        at = pl.multiple_of((chunk - plan.layers) * plan.chunk, 16)
        return [(buffer.at[pl.ds(0, rows), :], outs[0].at[pl.ds(at, rows), :])]

    shapes = [(plan.vocab, plan.dp * LANES)]
    return place_slabs(plan, slabs, plan.layers + first, count, shapes, store, held)[0]


def place_pieces(plan, pieces, held=()):
    owners = list(pieces)
    arrays = [array for owner in owners for array in pieces[owner]]
    rows, columns = arrays[0].shape
    downs, outs = plan.tp * 2 * plan.down_rows, plan.tp * 2 * plan.out_rows

    def body(*refs):
        sources, (down, out) = refs[: len(arrays)], refs[len(arrays) + len(held): -5]
        buffers, turned, loads, stores, out_stores = refs[-5:]
        dp = lax.axis_index("dp")
        core, x, y = dp % 2, (dp // 2) % 2, dp // 4

        def layer(n):
            flip_x, flip_y, flip_core = owners[n // plan.share]
            at = (y + flip_y * (1 - 2 * y)) * 4 + (x + flip_x * (1 - 2 * x)) * 2 + core + flip_core * (1 - 2 * core)
            return at * plan.share + n % plan.share

        loading = [pltpu.make_async_copy(source, buffers.at[n], loads.at[n]) for n, source in enumerate(sources)]
        storing = []
        for load in loading:
            load.start()
        for n, load in enumerate(loading):
            load.wait()
            storing.append(pltpu.make_async_copy(buffers.at[n, pl.ds(0, downs), :], down.at[layer(n)], stores.at[n]))
            storing[-1].start()
        for n in range(len(arrays)):
            for i in range(outs // LANES):
                for j in range(columns // LANES):
                    turned[n, pl.ds(j * LANES, LANES), pl.ds(i * LANES, LANES)] = buffers[
                        n, pl.ds(downs + i * LANES, LANES), pl.ds(j * LANES, LANES)
                    ].T
            storing.append(pltpu.make_async_copy(turned.at[n], out.at[layer(n)], out_stores.at[n]))
            storing[-1].start()
        for store in storing:
            store.wait()

    hbm = pl.BlockSpec(memory_space=pltpu.HBM)
    dma = pltpu.SemaphoreType.DMA((len(arrays),))
    shapes = [(plan.layers, downs, columns), (plan.layers, columns, outs)]
    return pl.pallas_call(
        body,
        out_shape=[jax.ShapeDtypeStruct(shape, jnp.bfloat16) for shape in shapes],
        in_specs=[hbm] * (len(arrays) + len(held)),
        out_specs=[hbm] * 2,
        scratch_shapes=[
            pltpu.VMEM((len(arrays), rows, columns), jnp.bfloat16),
            pltpu.VMEM((len(arrays), columns, outs), jnp.bfloat16),
            dma, dma, dma,
        ],
        input_output_aliases={len(arrays) + n: n for n in range(len(held))},
        cost_estimate=pl.CostEstimate(flops=10**7, bytes_accessed=4 * len(arrays) * rows * columns, transcendentals=0),
        compiler_params=pltpu.CompilerParams(vmem_limit_bytes=VMEM),
        name="place_pieces_end" if held else "place_pieces",
    )(*arrays, *held)


def solution(mesh):
    train_stack = P(None, ("dp", "tp"), None)
    train_head = P(("dp", "tp"), None)
    fused_stack = P(None, "tp", None)
    last_stack = P(None, None, "tp")
    head_rows = P("tp", None)

    def local_sync(w_query, w_key, w_value, w_out, w_gate, w_up, w_down, w_head):
        plan = Plan(mesh.shape["tp"], mesh.shape["dp"], w_query, w_gate, w_out, w_down, w_head)
        slabs, own_0, own_1 = gather(plan, w_query, w_key, w_value, w_out, w_gate, w_up, w_down, w_head)

        def swap(bit, array):
            return lax.ppermute(array, "dp", [(i, i ^ bit) for i in range(plan.dp)])

        pair, along_x, along_y = (functools.partial(swap, bit) for bit in (1, 2, 4))
        hold = lax.optimization_barrier

        x_1, y_0 = along_x(own_1), along_y(own_0)
        x_0, y_1 = along_x(own_0), along_y(own_1)
        pair_own = [pair(own_0), pair(own_1)]
        qkv_block, gate_up_block = place_layers(plan, slabs)
        x_1, y_0, qkv_block, slabs = hold((x_1, y_0, qkv_block, slabs))
        diagonal_0 = along_x(y_0)
        diagonal_1 = along_y(x_1)
        pair_x_1, pair_y_0 = pair(x_1), pair(y_0)
        early = plan.head_chunks // 2
        head_block = place_head(plan, slabs, early, plan.head_chunks - early)
        x_0, y_1, head_block, slabs = hold((x_0, y_1, head_block, slabs))
        pair_x_0, pair_y_1 = pair(x_0), pair(y_1)
        head_block = place_head(plan, slabs, 0, early, head_block)
        own_0, own_1, head_block = hold((own_0, own_1, head_block))
        near = {
            (0, 0, 0): [own_0, own_1], (0, 0, 1): pair_own, (1, 0, 0): [x_0, x_1], (1, 0, 1): [pair_x_0, pair_x_1],
            (0, 1, 0): [y_0, y_1], (0, 1, 1): [pair_y_0, pair_y_1],
        }
        placed = place_pieces(plan, near)
        diagonal_0, diagonal_1, down_block, o_block = hold((diagonal_0, diagonal_1, *placed))
        pair_diagonal = [pair(diagonal_0), pair(diagonal_1)]
        placed = place_pieces(plan, {(1, 1, 0): [diagonal_0, diagonal_1]}, (down_block, o_block))
        down_block, o_block = place_pieces(plan, {(1, 1, 1): pair_diagonal}, placed)
        return (
            qkv_block,
            o_block,
            gate_up_block,
            jnp.swapaxes(down_block, 1, 2),
            head_block,
        )

    return jax.shard_map(
        local_sync,
        mesh=mesh,
        in_specs=(train_stack,) * 7 + (train_head,),
        out_specs=(fused_stack, last_stack, fused_stack, last_stack, head_rows),
        check_vma=False,
    )
```

profile of v0, /device:TPU:0, one launch (start us, length us, event | category | flops | bytes accessed | tf_op | source)
XLA Modules:
  0.0 804.8 jit_solution(11806562481642797173)
XLA Ops:
  0.6 655.4 %gather.1 = (bf16[8,34,2176,128]{3,2,1,0:T(8,128)(2,1)}, bf16[960,1024]{1,0:T(8,128)(2,1)}, bf16[960,1024]{1,0:T(8,128)(2,1)}, bf16[8,120,1024]{2,1,0:T(8,128)(2,1)}, bf16[8,120,1024]{2,1,0:T(8,128)(2,1)}) custom-call(bf16[16,32,1024]{2,1,0:T(8,128)(2,1)} %q.1, bf16[16,32,1024]{2,1,0:T(8,128)(2,1)} %k.1, bf16[16,32,1024]{2,1,0:T(8,128)(2,1)} %v.1, ...), custom_call_target="tpu_custom_call" | custom-call | tf_op jit(solution)/shard_map/gather/pallas_call | solution.py:332
  656.0 1.5 collective-permute-start
  657.5 0.6 collective-permute-start.1
  658.1 1.5 collective-permute-start.4
  659.6 0.6 collective-permute-start.5
  660.1 45.5 %shard_map.119 = (bf16[16,768,1024]{2,1,0:T(8,128)(2,1)}, bf16[16,1408,1024]{2,1,0:T(8,128)(2,1)}) custom-call(bf16[8,34,2176,128]{3,2,1,0:T(8,128)(2,1)} %get-tuple-element.39.slab), custom_call_target="tpu_custom_call" | custom-call | flops 10000000 | bytes 142606336 | tf_op jit(solution)/shard_map/pallas_call | solution.py:399
  705.6 0.6 collective-permute-start.7
  706.2 24.4 %shard_map.120.refs_0_ = bf16[37984,1024]{1,0:T(8,128)(2,1)} custom-call(bf16[8,34,2176,128]{3,2,1,0:T(8,128)(2,1)} %get-tuple-element.39.slab), custom_call_target="tpu_custom_call" | custom-call | flops 10000000 | bytes 80216064 | tf_op jit(solution)/shard_map/pallas_call | solution.py:399
  730.6 12.8 %collective-permute-done.4.refs_4_ = bf16[960,1024]{1,0:T(8,128)(2,1)} collective-permute-done((bf16[960,1024]{1,0:T(8,128)(2,1)}, bf16[960,1024]{1,0:T(8,128)(2,1)}, u32[]{:S(2)}, u32[]{:S(2)}) %collective-permute-start.4) | collective-permute-done | bytes 1966112 | tf_op jit(solution)/shard_map/ppermute | solution.py:507
  743.4 1.2 collective-permute-done.5.refs_9_
  744.6 0.5 collective-permute-start.8
  745.1 0.0 collective-permute-start.10
  745.1 0.5 collective-permute-start.9
  745.6 0.6 collective-permute-start.2
  746.2 2.7 collective-permute-done.11.refs_11_
  748.9 0.6 collective-permute-start.3
  749.5 27.2 %shard_map.121 = bf16[37984,1024]{1,0:T(8,128)(2,1)} custom-call(bf16[8,34,2176,128]{3,2,1,0:T(8,128)(2,1)} %get-tuple-element.39.slab, bf16[37984,1024]{1,0:T(8,128)(2,1)} %shard_map.120.refs_0_), custom_call_target="tpu_custom_call", output_to_operand_aliasing={{}: (1, {})} | custom-call | flops 10000000 | bytes 80216064 | tf_op jit(solution)/shard_map/pallas_call | solution.py:399
  776.7 16.8 %place_pieces.1 = (bf16[16,704,1024]{2,1,0:T(8,128)(2,1)}, bf16[16,1024,256]{2,1,0:T(8,128)(2,1)}) custom-call(bf16[960,1024]{1,0:T(8,128)(2,1)} %get-tuple-element.41.refs_0_, bf16[960,1024]{1,0:T(8,128)(2,1)} %get-tuple-element.42.refs_1_, bf16[960,1024]{1,0:T(8,128)(2,1)} %collective-permute-done.6.refs_2_, ...), custom_call_target="tpu_custom_call" | custom-call | flops 10000000 | bytes 47185920 | tf_op jit(solution)/shard_map/place_pieces/pallas_call | solution.py:478
  793.5 0.6 collective-permute-done.3.refs_1_
  794.1 0.5 collective-permute-start.13
  794.6 3.6 place_pieces_end.2
  798.2 0.2 collective-permute-done.12.refs_0_
  798.4 2.8 collective-permute-done.13.refs_1_
  801.2 3.6 place_pieces_end.3
  (11 shorter events, 0.0 us)
Async XLA Ops:
  656.0 49.6 %collective-permute-start = (bf16[960,1024]{1,0:T(8,128)(2,1)}, bf16[960,1024]{1,0:T(8,128)(2,1)}, u32[]{:S(2)}, u32[]{:S(2)}) collective-permute-start(bf16[960,1024]{1,0:T(8,128)(2,1)} %get-tuple-element.42.refs_1_), channel_id=1, source_target_pairs={{0,2},{1,3},{2,0},{3,1},{4,6},{5,7},{6,4},{7,5},{8,10},{9,11},{10,... | collective-permute-start | bytes 5898248 | tf_op jit(solution)/shard_map/ppermute | solution.py:507
  657.5 48.7 %collective-permute-start.1 = (bf16[960,1024]{1,0:T(8,128)(2,1)}, bf16[960,1024]{1,0:T(8,128)(2,1)}, u32[]{:S(2)}, u32[]{:S(2)}) collective-permute-start(bf16[960,1024]{1,0:T(8,128)(2,1)} %get-tuple-element.41.refs_0_), channel_id=1, source_target_pairs={{0,4},{1,5},{2,6},{3,7},{4,0},{5,1},{6,2},{7,3},{8,12},{9,13},{10,... | collective-permute-start | bytes 5898248 | tf_op jit(solution)/shard_map/ppermute | solution.py:507
  658.1 85.3 %collective-permute-start.4 = (bf16[960,1024]{1,0:T(8,128)(2,1)}, bf16[960,1024]{1,0:T(8,128)(2,1)}, u32[]{:S(2)}, u32[]{:S(2)}) collective-permute-start(bf16[960,1024]{1,0:T(8,128)(2,1)} %get-tuple-element.41.refs_0_), channel_id=1, source_target_pairs={{0,2},{1,3},{2,0},{3,1},{4,6},{5,7},{6,4},{7,5},{8,10},{9,11},{10,... | collective-permute-start | bytes 5898248 | tf_op jit(solution)/shard_map/ppermute | solution.py:507
  659.6 85.0 %collective-permute-start.5 = (bf16[960,1024]{1,0:T(8,128)(2,1)}, bf16[960,1024]{1,0:T(8,128)(2,1)}, u32[]{:S(2)}, u32[]{:S(2)}) collective-permute-start(bf16[960,1024]{1,0:T(8,128)(2,1)} %get-tuple-element.42.refs_1_), channel_id=1, source_target_pairs={{0,4},{1,5},{2,6},{3,7},{4,0},{5,1},{6,2},{7,3},{8,12},{9,13},{10,... | collective-permute-start | bytes 5898248 | tf_op jit(solution)/shard_map/ppermute | solution.py:507
  660.1 84.9 %collective-permute-start.6 = (bf16[960,1024]{1,0:T(8,128)(2,1)}, bf16[960,1024]{1,0:T(8,128)(2,1)}, u32[]{:S(2)}, u32[]{:S(2)}) collective-permute-start(bf16[960,1024]{1,0:T(8,128)(2,1)} %get-tuple-element.41.refs_0_), channel_id=1, source_target_pairs={{0,1},{1,0},{2,3},{3,2},{4,5},{5,4},{6,7},{7,6},{8,9},{9,8},{10,11... | collective-permute-start | bytes 5898248 | tf_op jit(solution)/shard_map/ppermute | solution.py:507
  705.6 40.0 %collective-permute-start.7 = (bf16[960,1024]{1,0:T(8,128)(2,1)}, bf16[960,1024]{1,0:T(8,128)(2,1)}, u32[]{:S(2)}, u32[]{:S(2)}) collective-permute-start(bf16[960,1024]{1,0:T(8,128)(2,1)} %get-tuple-element.42.refs_1_), channel_id=1, source_target_pairs={{0,1},{1,0},{2,3},{3,2},{4,5},{5,4},{6,7},{7,6},{8,9},{9,8},{10,11... | collective-permute-start | bytes 5898248 | tf_op jit(solution)/shard_map/ppermute | solution.py:507
  744.6 4.3 collective-permute-start.11
  744.6 32.1 %collective-permute-start.8 = (bf16[960,1024]{1,0:T(8,128)(2,1)}, bf16[960,1024]{1,0:T(8,128)(2,1)}, u32[]{:S(2)}, u32[]{:S(2)}) collective-permute-start(bf16[960,1024]{1,0:T(8,128)(2,1)} %collective-permute-done.4.refs_4_), channel_id=1, source_target_pairs={{0,1},{1,0},{2,3},{3,2},{4,5},{5,4},{6,7},{7,6},{8,9},{9,8},{10,11... | collective-permute-start | bytes 5898248 | tf_op jit(solution)/shard_map/ppermute | solution.py:507
  745.1 31.6 %collective-permute-start.10 = (bf16[960,1024]{1,0:T(8,128)(2,1)}, bf16[960,1024]{1,0:T(8,128)(2,1)}, u32[]{:S(2)}, u32[]{:S(2)}) collective-permute-start(bf16[960,1024]{1,0:T(8,128)(2,1)} %collective-permute-done.1.refs_8_), channel_id=1, source_target_pairs={{0,1},{1,0},{2,3},{3,2},{4,5},{5,4},{6,7},{7,6},{8,9},{9,8},{10,11... | collective-permute-start | bytes 5898248 | tf_op jit(solution)/shard_map/ppermute | solution.py:507
  745.1 31.6 %collective-permute-start.9 = (bf16[960,1024]{1,0:T(8,128)(2,1)}, bf16[960,1024]{1,0:T(8,128)(2,1)}, u32[]{:S(2)}, u32[]{:S(2)}) collective-permute-start(bf16[960,1024]{1,0:T(8,128)(2,1)} %collective-permute-done.refs_5_), channel_id=1, source_target_pairs={{0,1},{1,0},{2,3},{3,2},{4,5},{5,4},{6,7},{7,6},{8,9},{9,8},{10,11... | collective-permute-start | bytes 5898248 | tf_op jit(solution)/shard_map/ppermute | solution.py:507
  745.6 47.8 %collective-permute-start.2 = (bf16[960,1024]{1,0:T(8,128)(2,1)}, bf16[960,1024]{1,0:T(8,128)(2,1)}, u32[]{:S(2)}, u32[]{:S(2)}) collective-permute-start(bf16[960,1024]{1,0:T(8,128)(2,1)} %collective-permute-done.1.refs_8_), channel_id=1, source_target_pairs={{0,2},{1,3},{2,0},{3,1},{4,6},{5,7},{6,4},{7,5},{8,10},{9,11},{10,... | collective-permute-start | bytes 5898248 | tf_op jit(solution)/shard_map/ppermute | solution.py:507
  748.9 45.2 %collective-permute-start.3 = (bf16[960,1024]{1,0:T(8,128)(2,1)}, bf16[960,1024]{1,0:T(8,128)(2,1)}, u32[]{:S(2)}, u32[]{:S(2)}) collective-permute-start(bf16[960,1024]{1,0:T(8,128)(2,1)} %collective-permute-done.refs_5_), channel_id=1, source_target_pairs={{0,4},{1,5},{2,6},{3,7},{4,0},{5,1},{6,2},{7,3},{8,12},{9,13},{10,... | collective-permute-start | bytes 5898248 | tf_op jit(solution)/shard_map/ppermute | solution.py:507
  794.1 4.3 collective-permute-start.12
  794.1 7.1 collective-permute-start.13
where the time goes:
time: 805 us
  Pallas kernels  776 us (96%)
  waiting for transfers between devices  20.3 us (3%)
    pallas_call x1, Pallas kernels, gather(): pl.pallas_call(functools.partial(gather_kernel, plan), out_shape=[jax.Sha...  655 us
    pallas_call x3, Pallas kernels, place_slabs(): pl.pallas_call(body, in_specs=[hbm] * (1 + len(held)), out_specs=[hbm] *...  97 us
    pallas_call x3, Pallas kernels, place_pieces(): pl.pallas_call(body, out_shape=[jax.ShapeDtypeStruct(shape, jnp.bfloat16)...  24 us
    ppermute x14, waiting for transfers between devices, swap(): return lax.ppermute(array, 'dp', [(i, i ^ bit) for i in range(plan.dp)])  20.3 us
  transfers between devices with their start and end apart: 14, of which 6 were waited for; matrix products, arithmetic and copies ran while one was open for 0% of the time, Pallas kernels for 15%

commit v1 on v0

--- a/solution.py
+++ b/solution.py
@@ -15,6 +15,7 @@
 BUFFERS = 6
 LAG = 2
 SHARE_AT = 14
+RETIRE = 8
 GROUP = 2
 
 
@@ -251,11 +252,30 @@
             for _, stop, final, n in pieces(source_dp, dp, place):
                 remote(stop, final, share_send.at[n], share_recv.at[n], tp=rank)
 
+    barrier = pltpu.get_barrier_semaphore()
+    peers = [{"tp": (z + step) % plan.tp} for step in range(1, plan.tp)]
+    peers += [{"dp": (dp + step) % plan.dp} for step in range(1, plan.dp)]
+    for peer in peers:
+        pl.semaphore_signal(barrier, inc=1, device_id=peer, device_id_type=MESH)
+    pl.semaphore_wait(barrier, len(peers))
+
     start_exchange(0)
     share_in_plane()
     for index in range(GROUP, AHEAD):
         start_exchange(index)
 
+    def retire(index):
+        finish(slab_view(index), index, chunk)
+
+        @pl.when((index < layers) & (index % GROUP == 0))
+        def _():
+            sent = pl.ds(0, (plan.tp - 1) * rows)
+            wait_for(zbuf.at[pl.ds(index, GROUP), sent, pl.ds(0, plan.layer_window)], z_send.at[index])
+
+        @pl.when(index >= layers)
+        def _():
+            finish_exchange(index, chunk)
+
     def step(index, _):
         slot = index % 2
 
@@ -284,6 +304,10 @@
         @pl.when(index >= 2 * LAG)
         def _():
             forward_diagonal(slab_view(index - 2 * LAG), index - 2 * LAG, chunk)
+
+        @pl.when(index >= RETIRE)
+        def _():
+            retire(index - RETIRE)
 
         return 0
 
@@ -298,21 +322,8 @@
         forward_diagonal(slab_view(index), index, chunk)
     forward_diagonal(slab_view(last), last, tail)
 
-    def drain(index, _):
-        finish(slab_view(index), index, chunk)
-
-        @pl.when((index < layers) & (index % GROUP == 0))
-        def _():
-            sent = pl.ds(0, (plan.tp - 1) * rows)
-            wait_for(zbuf.at[pl.ds(index, GROUP), sent, pl.ds(0, plan.layer_window)], z_send.at[index])
-
-        @pl.when(index >= layers)
-        def _():
-            finish_exchange(index, chunk)
-
-        return 0
-
-    lax.fori_loop(0, last, drain, 0)
+    for index in range(last - RETIRE, last):
+        retire(index)
     finish(slab_view(last), last, tail)
     finish_exchange(last, plan.tail_window)
     for n, own in enumerate((own_0, own_1)):
@@ -341,7 +352,7 @@
             per_chunk, per_chunk, per_chunk, per_chunk, per_chunk, per_chunk,
             dma((2, plan.dp)), dma((2,)), dma((2,)),
         ],
-        compiler_params=pltpu.CompilerParams(has_side_effects=True),
+        compiler_params=pltpu.CompilerParams(collective_id=0, has_side_effects=True),
         name="gather",
     )(*args)[:3]
 
@@ -517,7 +528,7 @@
         diagonal_0 = along_x(y_0)
         diagonal_1 = along_y(x_1)
         pair_x_1, pair_y_0 = pair(x_1), pair(y_0)
-        early = plan.head_chunks // 2
+        early = plan.head_chunks * 5 // 18
         head_block = place_head(plan, slabs, early, plan.head_chunks - early)
         x_0, y_1, head_block, slabs = hold((x_0, y_1, head_block, slabs))
         pair_x_0, pair_y_1 = pair(x_0), pair(y_1)

time: 805 us -> 802 us (level)
  transfers between devices with their start and end apart: 14 -> 14, of which waited for: 6 -> 7; matrix products, arithmetic and copies ran while one was open for 0% -> 0% of each run, Pallas kernels for 15% -> 15%
where the time goes in v1:
time: 802 us
  Pallas kernels  773 us (96%)
  waiting for transfers between devices  20.5 us (3%)
    pallas_call x1, Pallas kernels, gather(): pl.pallas_call(functools.partial(gather_kernel, plan), out_shape=[jax.Sha...  652 us
    pallas_call x3, Pallas kernels, place_slabs(): pl.pallas_call(body, in_specs=[hbm] * (1 + len(held)), out_specs=[hbm] *...  96.9 us
    pallas_call x3, Pallas kernels, place_pieces(): pl.pallas_call(body, out_shape=[jax.ShapeDtypeStruct(shape, jnp.bfloat16)...  24 us
    ppermute x14, waiting for transfers between devices, swap(): return lax.ppermute(array, 'dp', [(i, i ^ bit) for i in range(plan.dp)])  20.5 us
  transfers between devices with their start and end apart: 14, of which 7 were waited for; matrix products, arithmetic and copies ran while one was open for 0% of the time, Pallas kernels for 15%

profile of v1, /device:TPU:0, one launch (start us, length us, event | category | flops | bytes accessed | tf_op | source)
XLA Modules:
  0.0 802.0 jit_solution(9531031752910820058)
XLA Ops:
  0.6 652.5 %gather.1 = (bf16[8,34,2176,128]{3,2,1,0:T(8,128)(2,1)}, bf16[960,1024]{1,0:T(8,128)(2,1)}, bf16[960,1024]{1,0:T(8,128)(2,1)}, bf16[8,120,1024]{2,1,0:T(8,128)(2,1)}, bf16[8,120,1024]{2,1,0:T(8,128)(2,1)}) custom-call(bf16[16,32,1024]{2,1,0:T(8,128)(2,1)} %q.1, bf16[16,32,1024]{2,1,0:T(8,128)(2,1)} %k.1, bf16[16,32,1024]{2,1,0:T(8,128)(2,1)} %v.1, ...), custom_call_target="tpu_custom_call" | custom-call | tf_op jit(solution)/shard_map/gather/pallas_call | solution.py:343
  653.1 1.6 collective-permute-start
  654.6 0.6 collective-permute-start.1
  655.2 1.5 collective-permute-start.4
  656.7 0.5 collective-permute-start.5
  657.2 45.5 %shard_map.119 = (bf16[16,768,1024]{2,1,0:T(8,128)(2,1)}, bf16[16,1408,1024]{2,1,0:T(8,128)(2,1)}) custom-call(bf16[8,34,2176,128]{3,2,1,0:T(8,128)(2,1)} %get-tuple-element.39.slab), custom_call_target="tpu_custom_call" | custom-call | flops 10000000 | bytes 142606336 | tf_op jit(solution)/shard_map/pallas_call | solution.py:410
  702.7 0.6 collective-permute-start.7
  703.3 35.6 %shard_map.120.refs_0_ = bf16[37984,1024]{1,0:T(8,128)(2,1)} custom-call(bf16[8,34,2176,128]{3,2,1,0:T(8,128)(2,1)} %get-tuple-element.39.slab), custom_call_target="tpu_custom_call" | custom-call | flops 10000000 | bytes 115867648 | tf_op jit(solution)/shard_map/pallas_call | solution.py:410
  738.9 1.6 collective-permute-done.4.refs_4_
  740.5 1.2 collective-permute-done.5.refs_9_
  741.7 0.5 collective-permute-start.8
  742.2 0.5 collective-permute-start.9
  742.7 0.5 collective-permute-start.2
  743.2 2.8 collective-permute-done.11.refs_11_
  746.0 0.6 collective-permute-start.3
  746.6 15.9 %shard_map.121 = bf16[37984,1024]{1,0:T(8,128)(2,1)} custom-call(bf16[8,34,2176,128]{3,2,1,0:T(8,128)(2,1)} %get-tuple-element.39.slab, bf16[37984,1024]{1,0:T(8,128)(2,1)} %shard_map.120.refs_0_), custom_call_target="tpu_custom_call", output_to_operand_aliasing={{}: (1, {})} | custom-call | flops 10000000 | bytes 44564480 | tf_op jit(solution)/shard_map/pallas_call | solution.py:410
  762.4 16.8 %place_pieces.1 = (bf16[16,704,1024]{2,1,0:T(8,128)(2,1)}, bf16[16,1024,256]{2,1,0:T(8,128)(2,1)}) custom-call(bf16[960,1024]{1,0:T(8,128)(2,1)} %get-tuple-element.41.refs_0_, bf16[960,1024]{1,0:T(8,128)(2,1)} %get-tuple-element.42.refs_1_, bf16[960,1024]{1,0:T(8,128)(2,1)} %collective-permute-done.6.refs_2_, ...), custom_call_target="tpu_custom_call" | custom-call | flops 10000000 | bytes 47185920 | tf_op jit(solution)/shard_map/place_pieces/pallas_call | solution.py:489
  779.2 8.6 %collective-permute-done.2.refs_0_ = bf16[960,1024]{1,0:T(8,128)(2,1)} collective-permute-done((bf16[960,1024]{1,0:T(8,128)(2,1)}, bf16[960,1024]{1,0:T(8,128)(2,1)}, u32[]{:S(2)}, u32[]{:S(2)}) %collective-permute-start.2) | collective-permute-done | bytes 1966112 | tf_op jit(solution)/shard_map/ppermute | solution.py:518
  787.8 3.4 collective-permute-done.3.refs_1_
  791.2 0.5 collective-permute-start.13
  791.7 3.6 place_pieces_end.2
  795.3 0.2 collective-permute-done.12.refs_0_
  795.5 2.8 collective-permute-done.13.refs_1_
  798.3 3.6 place_pieces_end.3
  (11 shorter events, 0.0 us)
Async XLA Ops:
  653.1 49.6 %collective-permute-start = (bf16[960,1024]{1,0:T(8,128)(2,1)}, bf16[960,1024]{1,0:T(8,128)(2,1)}, u32[]{:S(2)}, u32[]{:S(2)}) collective-permute-start(bf16[960,1024]{1,0:T(8,128)(2,1)} %get-tuple-element.42.refs_1_), channel_id=1, source_target_pairs={{0,2},{1,3},{2,0},{3,1},{4,6},{5,7},{6,4},{7,5},{8,10},{9,11},{10,... | collective-permute-start | bytes 5898248 | tf_op jit(solution)/shard_map/ppermute | solution.py:518
  654.6 48.6 %collective-permute-start.1 = (bf16[960,1024]{1,0:T(8,128)(2,1)}, bf16[960,1024]{1,0:T(8,128)(2,1)}, u32[]{:S(2)}, u32[]{:S(2)}) collective-permute-start(bf16[960,1024]{1,0:T(8,128)(2,1)} %get-tuple-element.41.refs_0_), channel_id=1, source_target_pairs={{0,4},{1,5},{2,6},{3,7},{4,0},{5,1},{6,2},{7,3},{8,12},{9,13},{10,... | collective-permute-start | bytes 5898248 | tf_op jit(solution)/shard_map/ppermute | solution.py:518
  655.2 85.3 %collective-permute-start.4 = (bf16[960,1024]{1,0:T(8,128)(2,1)}, bf16[960,1024]{1,0:T(8,128)(2,1)}, u32[]{:S(2)}, u32[]{:S(2)}) collective-permute-start(bf16[960,1024]{1,0:T(8,128)(2,1)} %get-tuple-element.41.refs_0_), channel_id=1, source_target_pairs={{0,2},{1,3},{2,0},{3,1},{4,6},{5,7},{6,4},{7,5},{8,10},{9,11},{10,... | collective-permute-start | bytes 5898248 | tf_op jit(solution)/shard_map/ppermute | solution.py:518
  656.7 85.0 %collective-permute-start.5 = (bf16[960,1024]{1,0:T(8,128)(2,1)}, bf16[960,1024]{1,0:T(8,128)(2,1)}, u32[]{:S(2)}, u32[]{:S(2)}) collective-permute-start(bf16[960,1024]{1,0:T(8,128)(2,1)} %get-tuple-element.42.refs_1_), channel_id=1, source_target_pairs={{0,4},{1,5},{2,6},{3,7},{4,0},{5,1},{6,2},{7,3},{8,12},{9,13},{10,... | collective-permute-start | bytes 5898248 | tf_op jit(solution)/shard_map/ppermute | solution.py:518
  657.2 85.0 %collective-permute-start.6 = (bf16[960,1024]{1,0:T(8,128)(2,1)}, bf16[960,1024]{1,0:T(8,128)(2,1)}, u32[]{:S(2)}, u32[]{:S(2)}) collective-permute-start(bf16[960,1024]{1,0:T(8,128)(2,1)} %get-tuple-element.41.refs_0_), channel_id=1, source_target_pairs={{0,1},{1,0},{2,3},{3,2},{4,5},{5,4},{6,7},{7,6},{8,9},{9,8},{10,11... | collective-permute-start | bytes 5898248 | tf_op jit(solution)/shard_map/ppermute | solution.py:518
  702.7 40.0 %collective-permute-start.7 = (bf16[960,1024]{1,0:T(8,128)(2,1)}, bf16[960,1024]{1,0:T(8,128)(2,1)}, u32[]{:S(2)}, u32[]{:S(2)}) collective-permute-start(bf16[960,1024]{1,0:T(8,128)(2,1)} %get-tuple-element.42.refs_1_), channel_id=1, source_target_pairs={{0,1},{1,0},{2,3},{3,2},{4,5},{5,4},{6,7},{7,6},{8,9},{9,8},{10,11... | collective-permute-start | bytes 5898248 | tf_op jit(solution)/shard_map/ppermute | solution.py:518
  741.7 4.3 collective-permute-start.11
  741.7 20.7 %collective-permute-start.8 = (bf16[960,1024]{1,0:T(8,128)(2,1)}, bf16[960,1024]{1,0:T(8,128)(2,1)}, u32[]{:S(2)}, u32[]{:S(2)}) collective-permute-start(bf16[960,1024]{1,0:T(8,128)(2,1)} %collective-permute-done.4.refs_4_), channel_id=1, source_target_pairs={{0,1},{1,0},{2,3},{3,2},{4,5},{5,4},{6,7},{7,6},{8,9},{9,8},{10,11... | collective-permute-start | bytes 5898248 | tf_op jit(solution)/shard_map/ppermute | solution.py:518
  742.2 20.2 %collective-permute-start.10 = (bf16[960,1024]{1,0:T(8,128)(2,1)}, bf16[960,1024]{1,0:T(8,128)(2,1)}, u32[]{:S(2)}, u32[]{:S(2)}) collective-permute-start(bf16[960,1024]{1,0:T(8,128)(2,1)} %collective-permute-done.1.refs_8_), channel_id=1, source_target_pairs={{0,1},{1,0},{2,3},{3,2},{4,5},{5,4},{6,7},{7,6},{8,9},{9,8},{10,11... | collective-permute-start | bytes 5898248 | tf_op jit(solution)/shard_map/ppermute | solution.py:518
  742.2 20.2 %collective-permute-start.9 = (bf16[960,1024]{1,0:T(8,128)(2,1)}, bf16[960,1024]{1,0:T(8,128)(2,1)}, u32[]{:S(2)}, u32[]{:S(2)}) collective-permute-start(bf16[960,1024]{1,0:T(8,128)(2,1)} %collective-permute-done.refs_5_), channel_id=1, source_target_pairs={{0,1},{1,0},{2,3},{3,2},{4,5},{5,4},{6,7},{7,6},{8,9},{9,8},{10,11... | collective-permute-start | bytes 5898248 | tf_op jit(solution)/shard_map/ppermute | solution.py:518
  742.7 45.1 %collective-permute-start.2 = (bf16[960,1024]{1,0:T(8,128)(2,1)}, bf16[960,1024]{1,0:T(8,128)(2,1)}, u32[]{:S(2)}, u32[]{:S(2)}) collective-permute-start(bf16[960,1024]{1,0:T(8,128)(2,1)} %collective-permute-done.1.refs_8_), channel_id=1, source_target_pairs={{0,2},{1,3},{2,0},{3,1},{4,6},{5,7},{6,4},{7,5},{8,10},{9,11},{10,... | collective-permute-start | bytes 5898248 | tf_op jit(solution)/shard_map/ppermute | solution.py:518
  746.0 45.2 %collective-permute-start.3 = (bf16[960,1024]{1,0:T(8,128)(2,1)}, bf16[960,1024]{1,0:T(8,128)(2,1)}, u32[]{:S(2)}, u32[]{:S(2)}) collective-permute-start(bf16[960,1024]{1,0:T(8,128)(2,1)} %collective-permute-done.refs_5_), channel_id=1, source_target_pairs={{0,4},{1,5},{2,6},{3,7},{4,0},{5,1},{6,2},{7,3},{8,12},{9,13},{10,... | collective-permute-start | bytes 5898248 | tf_op jit(solution)/shard_map/ppermute | solution.py:518
  791.2 4.3 collective-permute-start.12
  791.2 7.1 collective-permute-start.13

commit v2 on v1

--- a/solution.py
+++ b/solution.py
@@ -16,6 +16,9 @@
 LAG = 2
 SHARE_AT = 14
 RETIRE = 8
+WHOLE = 3
+WHOLE_AT = 2
+PARTS = 4
 GROUP = 2
 
 
@@ -31,12 +34,21 @@
         self.wide_window = -(-self.wide // LANES) * LANES
         self.layer_window = 3 * self.part + 2 * self.wide_window
         self.head_chunks = -(-self.vocab // self.chunk)
-        self.tail = self.vocab - (self.head_chunks - 1) * self.chunk
         self.chunks = self.layers + self.head_chunks
-        self.tail_window = -(-(self.tail + LANES) // LANES) * LANES
+        end = self.vocab - (self.head_chunks - 1) * self.chunk
+        self.tail_window = -(-(end + LANES) // LANES) * LANES
         self.window_tiles = (self.head_chunks - 1) * self.chunk // LANES + self.tail_window // LANES
+        self.shift = max(self.vocab * r - self.head_base(r) * LANES for r in range(tp))
         self.out_rows, self.down_rows = w_out.shape[1], w_down.shape[1]
+        self.downs, self.outs = 2 * tp * self.down_rows, 2 * tp * self.out_rows
+        self.piece = self.downs + self.outs
         self.share = self.layers // dp
+        self.columns = w_out.shape[2]
+        self.whole = WHOLE * LANES
+        self.cut = self.columns - self.whole
+        self.extra_first = self.vocab - self.share * WHOLE * self.piece
+        self.ring = self.layers + self.extra_first // self.chunk
+        self.tail = self.extra_first % self.chunk
 
     def wide_base(self, rank):
         return (self.wide * rank) // LANES
@@ -46,8 +58,9 @@
         return base - (rank // (self.tp - 1)) * (self.vocab * (self.tp - 1) // LANES + self.window_tiles - self.head_tiles)
 
 
-def gather_kernel(plan, q, k, v, o, g, u, d, h, slabs, own_0, own_1, stop_0, stop_1, zbuf, tbuf, z_recv, z_send,
-                  local, x_recv, y_recv, a_recv, b_recv, pair_recv, send, stop_recv, share_recv, share_send):
+def gather_kernel(plan, q, k, v, o, g, u, d, h, slabs, own_0, own_1, whole, stop_0, stop_1, land_d, land_o, zbuf, tbuf,
+                  z_recv, z_send, local, x_recv, y_recv, a_recv, b_recv, pair_recv, send, stop_recv, share_recv,
+                  share_send, land_recv, land_send, whole_recv, whole_send, whole_pair_recv, whole_pair_send):
     z, dp = lax.axis_index("tp"), lax.axis_index("dp")
     core, x, y = dp % 2, (dp // 2) % 2, dp // 4
     x_peer = y * 4 + (1 - x) * 2 + core
@@ -55,7 +68,7 @@
     diagonal = (1 - y) * 4 + (1 - x) * 2 + core
     pair = dp + 1 - 2 * core
     rows, chunk, tail = plan.rows, plan.chunk, plan.tail
-    layers, last = plan.layers, plan.chunks - 1
+    layers, ring, last = plan.layers, plan.ring, plan.chunks - 1
     my_rows = pl.ds(pl.multiple_of(z * rows, rows), rows)
 
     def lanes(first_tile, width):
@@ -145,14 +158,7 @@
         def _():
             wait_exchange(index, chunk)
 
-        @pl.when(index < last - 1)
-        def _():
-            wait_exchange(index + 1, chunk)
-
-        @pl.when(index == last - 1)
-        def _():
-            wait_exchange(last, plan.tail_window)
-
+        wait_exchange(index + 1, chunk)
         tiles = chunk // LANES
         for tile in range(tiles):
             turn(slot, tile, index, tile)
@@ -160,10 +166,37 @@
             turn(slot, tiles + tile, index + 1, tile)
         store(slot, pl.multiple_of(head_shift, 16), index, 0, chunk)
 
+    def turn_rows(slot, first, count):
+        start = first // LANES
+        for tile in range(-(-(first % LANES + plan.shift + count) // LANES)):
+            at = start + tile
+            turn(slot, tile, layers + at // (chunk // LANES), at % (chunk // LANES))
+        return pl.multiple_of(first % LANES + head_shift, 16)
+
     def make_tail(slot):
-        for tile in range(plan.tail_window // LANES):
-            turn(slot, tile, last, tile)
-        store(slot, pl.multiple_of(head_shift, 16), last, 0, tail)
+        wait_exchange(ring + 1, chunk)
+        store(slot, turn_rows(slot, (ring - layers) * chunk, tail), ring, 0, tail)
+
+    def make_extra():
+        for index in range(ring + 2, last):
+            wait_exchange(index, chunk)
+        wait_exchange(last, plan.tail_window)
+        blocks = plan.share * WHOLE
+
+        def stored(n, own):
+            wait_for(own.at[:, pl.ds(plan.cut, LANES)], local.at[n % 2])
+
+        for n in range(blocks):
+            own = (own_0, own_1)[n // WHOLE]
+            if n >= 2:
+                stored(n, own)
+            at = turn_rows(n % 2, plan.extra_first + n * plan.piece, plan.piece)
+            pltpu.make_async_copy(
+                tbuf.at[n % 2, pl.ds(at, plan.piece), :],
+                own.at[:, pl.ds(plan.cut + n % WHOLE * LANES, LANES)], local.at[n % 2],
+            ).start()
+        for n in range(blocks - min(2, blocks), blocks):
+            stored(n, own_0)
 
 
     def slab_view(index):
@@ -203,15 +236,16 @@
 
 
     def pieces(source_dp, to, place):
-        all_rows = plan.tp * 2 * plan.down_rows
+        all_rows = plan.downs
         downs = pl.ds(pl.multiple_of(place * plan.down_rows, 8), plan.down_rows)
         outs = pl.ds(pl.multiple_of(all_rows + place * plan.out_rows, 8), plan.out_rows)
         stop_downs, stop_outs = pl.ds(0, plan.down_rows), pl.ds(plan.down_rows, plan.out_rows)
+        cut, home = pl.ds(plan.whole, plan.cut), pl.ds(0, plan.cut)
         found = []
         for n, (stop, own) in enumerate(((stop_0, own_0), (stop_1, own_1))):
             layer = to * 2 + n
-            found.append((d.at[layer], stop.at[source_dp, stop_downs, :], own.at[downs, :], n))
-            found.append((o.at[layer], stop.at[source_dp, stop_outs, :], own.at[outs, :], n))
+            found.append((d.at[layer, :, cut], stop.at[source_dp, stop_downs, :], own.at[downs, home], n))
+            found.append((o.at[layer, :, cut], stop.at[source_dp, stop_outs, :], own.at[outs, home], n))
         return found
 
     my_rank = dp // 2
@@ -251,6 +285,71 @@
                 wait_for(stop.at[source_dp], stop_recv.at[n, source_dp])
             for _, stop, final, n in pieces(source_dp, dp, place):
                 remote(stop, final, share_send.at[n], share_recv.at[n], tp=rank)
+
+
+    whole_columns = pl.ds(0, plan.whole)
+    mine = ((d, land_d, plan.down_rows, 0), (o, land_o, plan.out_rows, plan.downs))
+    half = layers // 2
+
+    def whole_out():
+        for n, (source, land, _, _) in enumerate(mine):
+            for to, at in ((x_peer, 0), (y_peer, 2)):
+                target = land.at[my_rank]
+                remote(source.at[:, :, whole_columns], target, land_send.at[n], land_recv.at[at + n], dp=to)
+
+    def whole_forward():
+        for owner, at, first, to, then in ((x_peer, 0, half, y_peer, 6), (y_peer, 2, 0, x_peer, 4)):
+            for n, (_, land, _, _) in enumerate(mine):
+                wait_for(land.at[owner // 2], land_recv.at[at + n])
+                part = land.at[owner // 2, pl.ds(first, half)]
+                remote(part, part, land_send.at[n], land_recv.at[then + n], dp=to)
+
+    def whole_arrive():
+        for first, at in ((0, 4), (half, 6)):
+            for n, (_, land, _, _) in enumerate(mine):
+                wait_for(land.at[diagonal // 2, pl.ds(first, half)], land_recv.at[at + n])
+
+    def whole_home(n, row):
+        _, _, count, first = mine[n]
+        return pl.ds(pl.multiple_of(first + row * count, 8), count)
+
+    def whole_to_rank(block, part):
+        flip_x, flip_y = block % 2, block // 2
+        rank = (y + flip_y * (1 - 2 * y)) * 2 + x + flip_x * (1 - 2 * x)
+        some = pl.ds(part * (layers // PARTS), layers // PARTS)
+
+        def move(sources):
+            for n, source in enumerate(sources):
+                target = whole.at[some, whole_home(n, core * plan.tp + z), :]
+
+                @pl.when(rank != z)
+                def _(source=source, target=target, n=n):
+                    remote(source, target, whole_send.at[n], whole_recv.at[n], tp=rank)
+
+                @pl.when(rank == z)
+                def _(source=source, target=target, n=n):
+                    pltpu.make_async_copy(source, target, whole_recv.at[n]).start()
+
+        pl.when(block == 0)(lambda: move([source.at[some, :, whole_columns] for source, _, _, _ in mine]))
+        pl.when(block != 0)(lambda: move([land.at[rank, some] for _, land, _, _ in mine]))
+
+    def whole_rows(which):
+        return [
+            whole.at[:, pl.ds(pl.multiple_of(first + which * plan.tp * count, 8), plan.tp * count), :]
+            for _, _, count, first in mine
+        ]
+
+    def whole_to_pair():
+        for n, part in enumerate(whole_rows(core)):
+            wait_for(part, whole_recv.at[n])
+            remote(part, part, whole_pair_send.at[n], whole_pair_recv.at[n], dp=pair)
+
+    def whole_finish():
+        for n, (_, land, count, first) in enumerate(mine):
+            wait_for(land.at[pl.ds(0, 3)], land_send.at[n])
+            wait_for(whole.at[:, pl.ds(first, (plan.tp - 1) * count), :], whole_send.at[n])
+            wait_for(whole_rows(core)[n], whole_pair_send.at[n])
+            wait_for(whole_rows(1 - core)[n], whole_pair_recv.at[n])
 
     barrier = pltpu.get_barrier_semaphore()
     peers = [{"tp": (z + step) % plan.tp} for step in range(1, plan.tp)]
@@ -260,6 +359,7 @@
     pl.semaphore_wait(barrier, len(peers))
 
     start_exchange(0)
+    whole_out()
     share_in_plane()
     for index in range(GROUP, AHEAD):
         start_exchange(index)
@@ -287,6 +387,22 @@
         def _():
             share_to_rank((index - SHARE_AT) // 2)
 
+        @pl.when(index == WHOLE_AT)
+        def _():
+            whole_forward()
+
+        @pl.when(index == WHOLE_AT + 3)
+        def _():
+            whole_arrive()
+
+        @pl.when((index >= WHOLE_AT) & (index < WHOLE_AT + 4 * PARTS))
+        def _():
+            whole_to_rank((index - WHOLE_AT) // PARTS, (index - WHOLE_AT) % PARTS)
+
+        @pl.when(index == ring - 2)
+        def _():
+            whole_to_pair()
+
         @pl.when(index < layers)
         def _():
             make_layer(index, slot)
@@ -311,35 +427,40 @@
 
         return 0
 
-    lax.fori_loop(0, last, step, 0)
-
-    make_tail(last % 2)
-    send_own(slab_view(last), last, last % 2, tail)
-    for index in range(last - LAG, last):
+    lax.fori_loop(0, ring, step, 0)
+
+    make_tail(ring % 2)
+    send_own(slab_view(ring), ring, ring % 2, tail)
+    make_extra()
+    for index in range(ring - LAG, ring):
         forward(slab_view(index), index, chunk)
-    forward(slab_view(last), last, tail)
-    for index in range(last - 2 * LAG, last):
+    forward(slab_view(ring), ring, tail)
+    for index in range(ring - 2 * LAG, ring):
         forward_diagonal(slab_view(index), index, chunk)
-    forward_diagonal(slab_view(last), last, tail)
-
-    for index in range(last - RETIRE, last):
+    forward_diagonal(slab_view(ring), ring, tail)
+
+    for index in range(ring - RETIRE, ring):
         retire(index)
-    finish(slab_view(last), last, tail)
+    finish(slab_view(ring), ring, tail)
+    for index in range(ring, last):
+        finish_exchange(index, chunk)
     finish_exchange(last, plan.tail_window)
+    whole_finish()
     for n, own in enumerate((own_0, own_1)):
-        wait_for(own, share_recv.at[n])
+        wait_for(own.at[:, pl.ds(0, plan.cut)], share_recv.at[n])
         for parts in (8, 5):
-            wait_for(own.at[pl.ds(0, parts * (plan.down_rows + plan.out_rows)), :], share_send.at[n])
+            sent = pl.ds(0, parts * (plan.down_rows + plan.out_rows))
+            wait_for(own.at[sent, pl.ds(0, plan.cut)], share_send.at[n])
 
 
 def gather(plan, *args):
     dma = pltpu.SemaphoreType.DMA
     per_chunk = dma((plan.chunks,))
-    columns = args[3].shape[2]
     share_rows = plan.down_rows + plan.out_rows
     hbm = pl.BlockSpec(memory_space=pltpu.HBM)
-    shapes = [(plan.dp, plan.chunks, plan.chunk, LANES)]
-    shapes += [(plan.tp * 2 * share_rows, columns)] * 2 + [(plan.dp, share_rows, columns)] * 2
+    shapes = [(plan.dp, plan.ring + 1, plan.chunk, LANES), (plan.piece, plan.columns), (plan.piece, plan.columns)]
+    shapes += [(plan.layers, plan.piece, plan.whole)] + [(plan.dp, share_rows, plan.cut)] * 2
+    shapes += [(plan.tp, plan.layers, count, plan.whole) for count in (plan.down_rows, plan.out_rows)]
     return pl.pallas_call(
         functools.partial(gather_kernel, plan),
         out_shape=[jax.ShapeDtypeStruct(shape, jnp.bfloat16) for shape in shapes],
@@ -351,10 +472,11 @@
             per_chunk, per_chunk, dma((2,)),
             per_chunk, per_chunk, per_chunk, per_chunk, per_chunk, per_chunk,
             dma((2, plan.dp)), dma((2,)), dma((2,)),
+            dma((8,)), dma((2,)), dma((2,)), dma((2,)), dma((2,)), dma((2,)),
         ],
         compiler_params=pltpu.CompilerParams(collective_id=0, has_side_effects=True),
         name="gather",
-    )(*args)[:3]
+    )(*args)[:4]
 
 
 def place_slabs(plan, slabs, first, count, shapes, store, held=()):
@@ -366,9 +488,9 @@
         outs, (buffers, loads, stores) = refs[len(held):-3], refs[-3:]
 
         def each_size(chunk, act):
-            if first + count == plan.chunks:
-                pl.when(chunk < plan.chunks - 1)(lambda: act(plan.chunk))
-                pl.when(chunk == plan.chunks - 1)(lambda: act(plan.tail))
+            if first + count > plan.ring:
+                pl.when(chunk < plan.ring)(lambda: act(plan.chunk))
+                pl.when(chunk == plan.ring)(lambda: act(plan.tail))
             else:
                 act(plan.chunk)
 
@@ -447,60 +569,92 @@
     return place_slabs(plan, slabs, plan.layers + first, count, shapes, store, held)[0]
 
 
-def place_pieces(plan, pieces, held=()):
-    owners = list(pieces)
-    arrays = [array for owner in owners for array in pieces[owner]]
-    rows, columns = arrays[0].shape
-    downs, outs = plan.tp * 2 * plan.down_rows, plan.tp * 2 * plan.out_rows
+def place_rows(plan, arrays, spots, width, column, held):
+    count = len(spots([array for array in arrays], 0))
+    columns = arrays[0].shape[-1]
+    outs = [
+        jax.ShapeDtypeStruct((plan.layers, plan.downs, plan.columns), jnp.bfloat16),
+        jax.ShapeDtypeStruct((plan.layers, plan.columns, plan.outs), jnp.bfloat16),
+        jax.ShapeDtypeStruct((plan.vocab, plan.dp * LANES), jnp.bfloat16),
+    ]
+    with_head = columns > width
+    kept = [n for n in range(3) if n in held]
+    made = [n for n in range(3 if with_head else 2)]
 
     def body(*refs):
-        sources, (down, out) = refs[: len(arrays)], refs[len(arrays) + len(held): -5]
-        buffers, turned, loads, stores, out_stores = refs[-5:]
-        dp = lax.axis_index("dp")
-        core, x, y = dp % 2, (dp // 2) % 2, dp // 4
-
-        def layer(n):
-            flip_x, flip_y, flip_core = owners[n // plan.share]
-            at = (y + flip_y * (1 - 2 * y)) * 4 + (x + flip_x * (1 - 2 * x)) * 2 + core + flip_core * (1 - 2 * core)
-            return at * plan.share + n % plan.share
-
-        loading = [pltpu.make_async_copy(source, buffers.at[n], loads.at[n]) for n, source in enumerate(sources)]
+        targets = dict(zip(made, refs[len(arrays) + len(kept):-6], strict=True))
+        buffers, turned, loads, stores, out_stores, head_stores = refs[-6:]
+        moves = spots(refs[: len(arrays)], lax.axis_index("dp"))
+        loading = [pltpu.make_async_copy(move[0], buffers.at[n], loads.at[n]) for n, move in enumerate(moves)]
         storing = []
         for load in loading:
             load.start()
-        for n, load in enumerate(loading):
+
+        def put(source, target, sem):
+            storing.append(pltpu.make_async_copy(source, target, sem))
+            storing[-1].start()
+
+        place = pl.ds(column, width)
+        for n, (load, (_, layer, owner, part)) in enumerate(zip(loading, moves, strict=True)):
             load.wait()
-            storing.append(pltpu.make_async_copy(buffers.at[n, pl.ds(0, downs), :], down.at[layer(n)], stores.at[n]))
-            storing[-1].start()
-        for n in range(len(arrays)):
-            for i in range(outs // LANES):
-                for j in range(columns // LANES):
+            put(buffers.at[n, pl.ds(0, plan.downs), pl.ds(0, width)], targets[0].at[layer, :, place], stores.at[n])
+            for j in range((columns - width) // LANES):
+                row = plan.extra_first + (part * WHOLE + j) * plan.piece
+                put(
+                    buffers.at[n, :, pl.ds(width + j * LANES, LANES)],
+                    targets[2].at[pl.ds(row, plan.piece), pl.ds(pl.multiple_of(owner * LANES, LANES), LANES)],
+                    head_stores.at[n, j],
+                )
+        for n, (_, layer, _, _) in enumerate(moves):
+            for i in range(plan.outs // LANES):
+                for j in range(width // LANES):
                     turned[n, pl.ds(j * LANES, LANES), pl.ds(i * LANES, LANES)] = buffers[
-                        n, pl.ds(downs + i * LANES, LANES), pl.ds(j * LANES, LANES)
+                        n, pl.ds(plan.downs + i * LANES, LANES), pl.ds(j * LANES, LANES)
                     ].T
-            storing.append(pltpu.make_async_copy(turned.at[n], out.at[layer(n)], out_stores.at[n]))
-            storing[-1].start()
+            put(turned.at[n], targets[1].at[layer, place, :], out_stores.at[n])
         for store in storing:
             store.wait()
 
     hbm = pl.BlockSpec(memory_space=pltpu.HBM)
-    dma = pltpu.SemaphoreType.DMA((len(arrays),))
-    shapes = [(plan.layers, downs, columns), (plan.layers, columns, outs)]
-    return pl.pallas_call(
+    dma = pltpu.SemaphoreType.DMA((count,))
+    result = pl.pallas_call(
         body,
-        out_shape=[jax.ShapeDtypeStruct(shape, jnp.bfloat16) for shape in shapes],
-        in_specs=[hbm] * (len(arrays) + len(held)),
-        out_specs=[hbm] * 2,
+        out_shape=[outs[n] for n in made],
+        in_specs=[hbm] * (len(arrays) + len(kept)),
+        out_specs=[hbm] * len(made),
         scratch_shapes=[
-            pltpu.VMEM((len(arrays), rows, columns), jnp.bfloat16),
-            pltpu.VMEM((len(arrays), columns, outs), jnp.bfloat16),
-            dma, dma, dma,
+            pltpu.VMEM((count, plan.piece, columns), jnp.bfloat16),
+            pltpu.VMEM((count, width, plan.outs), jnp.bfloat16),
+            dma, dma, dma, pltpu.SemaphoreType.DMA((count, max(WHOLE, 1))),
         ],
-        input_output_aliases={len(arrays) + n: n for n in range(len(held))},
-        cost_estimate=pl.CostEstimate(flops=10**7, bytes_accessed=4 * len(arrays) * rows * columns, transcendentals=0),
+        input_output_aliases={len(arrays) + i: n for i, n in enumerate(kept)},
+        cost_estimate=pl.CostEstimate(flops=10**7, bytes_accessed=4 * count * plan.piece * columns, transcendentals=0),
         compiler_params=pltpu.CompilerParams(vmem_limit_bytes=VMEM),
-        name="place_pieces_end" if held else "place_pieces",
-    )(*arrays, *held)
+    )(*arrays, *(held[n] for n in kept))
+    return dict(zip(made, result, strict=True))
+
+
+def place_whole(plan, whole):
+    def spots(refs, dp):
+        return [(refs[0].at[layer], layer, 0, 0) for layer in range(plan.layers)]
+
+    return place_rows(plan, [whole], spots, plan.whole, 0, {})
+
+
+def place_shares(plan, shares, held):
+    owners = list(shares)
+    arrays = [array for owner in owners for array in shares[owner]]
+
+    def spots(refs, dp):
+        core, x, y = dp % 2, (dp // 2) % 2, dp // 4
+        found = []
+        for n, ref in enumerate(refs):
+            flip_x, flip_y, flip_core = owners[n // plan.share]
+            owner = (y + flip_y * (1 - 2 * y)) * 4 + (x + flip_x * (1 - 2 * x)) * 2 + core + flip_core * (1 - 2 * core)
+            found.append((ref, owner * plan.share + n % plan.share, owner, n % plan.share))
+        return found
+
+    return place_rows(plan, arrays, spots, plan.cut, plan.whole, held)
 
 
 def solution(mesh):
@@ -512,7 +666,7 @@
 
     def local_sync(w_query, w_key, w_value, w_out, w_gate, w_up, w_down, w_head):
         plan = Plan(mesh.shape["tp"], mesh.shape["dp"], w_query, w_gate, w_out, w_down, w_head)
-        slabs, own_0, own_1 = gather(plan, w_query, w_key, w_value, w_out, w_gate, w_up, w_down, w_head)
+        slabs, own_0, own_1, whole = gather(plan, w_query, w_key, w_value, w_out, w_gate, w_up, w_down, w_head)
 
         def swap(bit, array):
             return lax.ppermute(array, "dp", [(i, i ^ bit) for i in range(plan.dp)])
@@ -528,21 +682,25 @@
         diagonal_0 = along_x(y_0)
         diagonal_1 = along_y(x_1)
         pair_x_1, pair_y_0 = pair(x_1), pair(y_0)
-        early = plan.head_chunks * 5 // 18
-        head_block = place_head(plan, slabs, early, plan.head_chunks - early)
-        x_0, y_1, head_block, slabs = hold((x_0, y_1, head_block, slabs))
+        head_chunks = plan.ring + 1 - plan.layers
+        early = head_chunks // 4
+        head_block = place_head(plan, slabs, early, head_chunks - early)
+        x_0, y_1, head_block, slabs, whole = hold((x_0, y_1, head_block, slabs, whole))
         pair_x_0, pair_y_1 = pair(x_0), pair(y_1)
+        placed = place_whole(plan, whole)
+        slabs, *placed = hold((slabs, placed[0], placed[1]))
         head_block = place_head(plan, slabs, 0, early, head_block)
         own_0, own_1, head_block = hold((own_0, own_1, head_block))
         near = {
             (0, 0, 0): [own_0, own_1], (0, 0, 1): pair_own, (1, 0, 0): [x_0, x_1], (1, 0, 1): [pair_x_0, pair_x_1],
             (0, 1, 0): [y_0, y_1], (0, 1, 1): [pair_y_0, pair_y_1],
         }
-        placed = place_pieces(plan, near)
-        diagonal_0, diagonal_1, down_block, o_block = hold((diagonal_0, diagonal_1, *placed))
+        placed = place_shares(plan, near, {0: placed[0], 1: placed[1], 2: head_block})
+        diagonal_0, diagonal_1, *placed = hold((diagonal_0, diagonal_1, placed[0], placed[1], placed[2]))
         pair_diagonal = [pair(diagonal_0), pair(diagonal_1)]
-        placed = place_pieces(plan, {(1, 1, 0): [diagonal_0, diagonal_1]}, (down_block, o_block))
-        down_block, o_block = place_pieces(plan, {(1, 1, 1): pair_diagonal}, placed)
+        placed = place_shares(plan, {(1, 1, 0): [diagonal_0, diagonal_1]}, dict(enumerate(placed)))
+        placed = place_shares(plan, {(1, 1, 1): pair_diagonal}, placed)
+        down_block, o_block, head_block = placed[0], placed[1], placed[2]
         return (
             qkv_block,
             o_block,

time: 802 us -> 907 us (1.13)
  Pallas kernels: 773 us -> 880 us
    pallas_call x1, Pallas kernels: 652 us -> 757 us  [gather(): pl.pallas_call(functools.partial(gather_kernel, plan), out_shape=[jax.Sha...]
    pallas_call x3 -> x4, Pallas kernels: 24 us -> 33.4 us  [place_rows(): pl.pallas_call(body, out_shape=[outs[n] for n in made], in_specs=[hbm] *...]
  transfers between devices with their start and end apart: 14 -> 14, of which waited for: 7 -> 7; matrix products, arithmetic and copies ran while one was open for 0% -> 0% of each run, Pallas kernels for 15% -> 13%
where the time goes in v2:
time: 907 us
  Pallas kernels  880 us (97%)
  waiting for transfers between devices  18.9 us (2%)
    pallas_call x1, Pallas kernels, gather(): pl.pallas_call(functools.partial(gather_kernel, plan), out_shape=[jax.Sha...  757 us
    pallas_call x3, Pallas kernels, place_slabs(): pl.pallas_call(body, in_specs=[hbm] * (1 + len(held)), out_specs=[hbm] *...  89.8 us
    pallas_call x4, Pallas kernels, place_rows(): pl.pallas_call(body, out_shape=[outs[n] for n in made], in_specs=[hbm] *...  33.4 us
    ppermute x14, waiting for transfers between devices, swap(): return lax.ppermute(array, 'dp', [(i, i ^ bit) for i in range(plan.dp)])  18.9 us
  transfers between devices with their start and end apart: 14, of which 7 were waited for; matrix products, arithmetic and copies ran while one was open for 0% of the time, Pallas kernels for 13%

profile of v2, /device:TPU:0, one launch (start us, length us, event | category | flops | bytes accessed | tf_op | source)
XLA Modules:
  0.0 906.7 jit_solution(6001965080566070311)
XLA Ops:
  0.6 756.9 %gather.1 = (bf16[8,31,2176,128]{3,2,1,0:T(8,128)(2,1)}, bf16[960,1024]{1,0:T(8,128)(2,1)}, bf16[960,1024]{1,0:T(8,128)(2,1)}, bf16[16,960,384]{2,1,0:T(8,128)(2...) custom-call(bf16[16,32,1024]{2,1,0:T(8,128)(2,1)} %q.1, ...), custom_call_target="tpu_custom_call" | custom-call | tf_op jit(solution)/shard_map/gather/pallas_call | solution.py:464
  757.6 1.8 collective-permute-start
  759.4 0.2 collective-permute-start.1
  759.6 1.8 collective-permute-start.4
  761.4 0.3 collective-permute-start.5
  761.7 45.5 %shard_map.119 = (bf16[16,768,1024]{2,1,0:T(8,128)(2,1)}, bf16[16,1408,1024]{2,1,0:T(8,128)(2,1)}) custom-call(bf16[8,31,2176,128]{3,2,1,0:T(8,128)(2,1)} %get-tuple-element.55.slab), custom_call_target="tpu_custom_call" | custom-call | flops 10000000 | bytes 142606336 | tf_op jit(solution)/shard_map/pallas_call | solution.py:532
  807.2 0.6 collective-permute-start.7
  807.7 34.0 %shard_map.120.refs_0_ = bf16[37984,1024]{1,0:T(8,128)(2,1)} custom-call(bf16[8,31,2176,128]{3,2,1,0:T(8,128)(2,1)} %get-tuple-element.55.slab), custom_call_target="tpu_custom_call" | custom-call | flops 10000000 | bytes 106954752 | tf_op jit(solution)/shard_map/pallas_call | solution.py:532
  841.7 3.2 collective-permute-done.4.refs_4_
  845.0 1.5 collective-permute-done.5.refs_9_
  846.4 0.5 collective-permute-start.8
  847.0 0.5 collective-permute-start.9
  847.5 0.4 collective-permute-start.2
  847.8 2.9 collective-permute-done.11.refs_11_
  850.8 0.3 collective-permute-start.3
  851.1 9.4 %shard_map.121 = (bf16[16,704,1024]{2,1,0:T(8,128)(2,1)}, bf16[16,1024,256]{2,1,0:T(8,128)(2,1)}) custom-call(bf16[16,960,384]{2,1,0:T(8,128)(2,1)} %get-tuple-element.52.refs_0_), custom_call_target="tpu_custom_call" | custom-call | flops 10000000 | bytes 23592960 | tf_op jit(solution)/shard_map/pallas_call | solution.py:620
  860.5 10.4 %shard_map.122.refs_14_ = bf16[37984,1024]{1,0:T(8,128)(2,1)} custom-call(bf16[8,31,2176,128]{3,2,1,0:T(8,128)(2,1)} %get-tuple-element.55.slab, bf16[37984,1024]{1,0:T(8,128)(2,1)} %shard_map.120.refs_0_), custom_call_target="tpu_custom_call", output_to_operand_aliasing={{}: (1, {})} | custom-call | flops 10000000 | bytes 26738688 | tf_op jit(solution)/shard_map/pallas_call | solution.py:532
  870.9 16.8 %shard_map.123 = (bf16[16,704,1024]{2,1,0:T(8,128)(2,1)}, bf16[16,1024,256]{2,1,0:T(8,128)(2,1)}, bf16[37984,1024]{1,0:T(8,128)(2,1)}) custom-call(bf16[960,1024]{1,0:T(8,128)(2,1)} %get-tuple-element.57.refs_0_, bf16[960,1024]{1,0:T(8,128)(2,1)} %get-tuple-element.58.refs_1_, ...), custom_call_target="tpu_custom_call", output_to_operand_aliasing={{0}: (12, {}), {1}: (13, {}), {2}: (14, {})} | custom-call | flops 10000000 | bytes 47185920 | tf_op jit(solution)/shard_map/pallas_call | solution.py:620
  887.7 4.9 collective-permute-done.2.refs_0_
  892.6 3.4 collective-permute-done.3.refs_1_
  895.9 0.5 collective-permute-start.13
  896.4 3.6 shard_map.124
  900.2 2.8 collective-permute-done.13.refs_1_
  903.1 3.6 shard_map.125
  (12 shorter events, 0.2 us)
Async XLA Ops:
  757.6 49.6 %collective-permute-start = (bf16[960,1024]{1,0:T(8,128)(2,1)}, bf16[960,1024]{1,0:T(8,128)(2,1)}, u32[]{:S(2)}, u32[]{:S(2)}) collective-permute-start(bf16[960,1024]{1,0:T(8,128)(2,1)} %get-tuple-element.58.refs_1_), channel_id=1, source_target_pairs={{0,2},{1,3},{2,0},{3,1},{4,6},{5,7},{6,4},{7,5},{8,10},{9,11},{10,... | collective-permute-start | bytes 5898248 | tf_op jit(solution)/shard_map/ppermute | solution.py:672
  759.4 48.3 %collective-permute-start.1 = (bf16[960,1024]{1,0:T(8,128)(2,1)}, bf16[960,1024]{1,0:T(8,128)(2,1)}, u32[]{:S(2)}, u32[]{:S(2)}) collective-permute-start(bf16[960,1024]{1,0:T(8,128)(2,1)} %get-tuple-element.57.refs_0_), channel_id=1, source_target_pairs={{0,4},{1,5},{2,6},{3,7},{4,0},{5,1},{6,2},{7,3},{8,12},{9,13},{10,... | collective-permute-start | bytes 5898248 | tf_op jit(solution)/shard_map/ppermute | solution.py:672
  759.6 85.4 %collective-permute-start.4 = (bf16[960,1024]{1,0:T(8,128)(2,1)}, bf16[960,1024]{1,0:T(8,128)(2,1)}, u32[]{:S(2)}, u32[]{:S(2)}) collective-permute-start(bf16[960,1024]{1,0:T(8,128)(2,1)} %get-tuple-element.57.refs_0_), channel_id=1, source_target_pairs={{0,2},{1,3},{2,0},{3,1},{4,6},{5,7},{6,4},{7,5},{8,10},{9,11},{10,... | collective-permute-start | bytes 5898248 | tf_op jit(solution)/shard_map/ppermute | solution.py:672
  761.4 85.0 %collective-permute-start.5 = (bf16[960,1024]{1,0:T(8,128)(2,1)}, bf16[960,1024]{1,0:T(8,128)(2,1)}, u32[]{:S(2)}, u32[]{:S(2)}) collective-permute-start(bf16[960,1024]{1,0:T(8,128)(2,1)} %get-tuple-element.58.refs_1_), channel_id=1, source_target_pairs={{0,4},{1,5},{2,6},{3,7},{4,0},{5,1},{6,2},{7,3},{8,12},{9,13},{10,... | collective-permute-start | bytes 5898248 | tf_op jit(solution)/shard_map/ppermute | solution.py:672
  761.7 85.3 %collective-permute-start.6 = (bf16[960,1024]{1,0:T(8,128)(2,1)}, bf16[960,1024]{1,0:T(8,128)(2,1)}, u32[]{:S(2)}, u32[]{:S(2)}) collective-permute-start(bf16[960,1024]{1,0:T(8,128)(2,1)} %get-tuple-element.57.refs_0_), channel_id=1, source_target_pairs={{0,1},{1,0},{2,3},{3,2},{4,5},{5,4},{6,7},{7,6},{8,9},{9,8},{10,11... | collective-permute-start | bytes 5898248 | tf_op jit(solution)/shard_map/ppermute | solution.py:672
  807.2 40.3 %collective-permute-start.7 = (bf16[960,1024]{1,0:T(8,128)(2,1)}, bf16[960,1024]{1,0:T(8,128)(2,1)}, u32[]{:S(2)}, u32[]{:S(2)}) collective-permute-start(bf16[960,1024]{1,0:T(8,128)(2,1)} %get-tuple-element.58.refs_1_), channel_id=1, source_target_pairs={{0,1},{1,0},{2,3},{3,2},{4,5},{5,4},{6,7},{7,6},{8,9},{9,8},{10,11... | collective-permute-start | bytes 5898248 | tf_op jit(solution)/shard_map/ppermute | solution.py:672
  846.4 4.3 collective-permute-start.11
  846.4 24.4 %collective-permute-start.8 = (bf16[960,1024]{1,0:T(8,128)(2,1)}, bf16[960,1024]{1,0:T(8,128)(2,1)}, u32[]{:S(2)}, u32[]{:S(2)}) collective-permute-start(bf16[960,1024]{1,0:T(8,128)(2,1)} %collective-permute-done.4.refs_4_), channel_id=1, source_target_pairs={{0,1},{1,0},{2,3},{3,2},{4,5},{5,4},{6,7},{7,6},{8,9},{9,8},{10,11... | collective-permute-start | bytes 5898248 | tf_op jit(solution)/shard_map/ppermute | solution.py:672
  846.9 23.9 %collective-permute-start.10 = (bf16[960,1024]{1,0:T(8,128)(2,1)}, bf16[960,1024]{1,0:T(8,128)(2,1)}, u32[]{:S(2)}, u32[]{:S(2)}) collective-permute-start(bf16[960,1024]{1,0:T(8,128)(2,1)} %collective-permute-done.1.refs_8_), channel_id=1, source_target_pairs={{0,1},{1,0},{2,3},{3,2},{4,5},{5,4},{6,7},{7,6},{8,9},{9,8},{10,11... | collective-permute-start | bytes 5898248 | tf_op jit(solution)/shard_map/ppermute | solution.py:672
  847.0 23.9 %collective-permute-start.9 = (bf16[960,1024]{1,0:T(8,128)(2,1)}, bf16[960,1024]{1,0:T(8,128)(2,1)}, u32[]{:S(2)}, u32[]{:S(2)}) collective-permute-start(bf16[960,1024]{1,0:T(8,128)(2,1)} %collective-permute-done.refs_5_), channel_id=1, source_target_pairs={{0,1},{1,0},{2,3},{3,2},{4,5},{5,4},{6,7},{7,6},{8,9},{9,8},{10,11... | collective-permute-start | bytes 5898248 | tf_op jit(solution)/shard_map/ppermute | solution.py:672
  847.5 45.1 %collective-permute-start.2 = (bf16[960,1024]{1,0:T(8,128)(2,1)}, bf16[960,1024]{1,0:T(8,128)(2,1)}, u32[]{:S(2)}, u32[]{:S(2)}) collective-permute-start(bf16[960,1024]{1,0:T(8,128)(2,1)} %collective-permute-done.1.refs_8_), channel_id=1, source_target_pairs={{0,2},{1,3},{2,0},{3,1},{4,6},{5,7},{6,4},{7,5},{8,10},{9,11},{10,... | collective-permute-start | bytes 5898248 | tf_op jit(solution)/shard_map/ppermute | solution.py:672
  850.8 45.2 %collective-permute-start.3 = (bf16[960,1024]{1,0:T(8,128)(2,1)}, bf16[960,1024]{1,0:T(8,128)(2,1)}, u32[]{:S(2)}, u32[]{:S(2)}) collective-permute-start(bf16[960,1024]{1,0:T(8,128)(2,1)} %collective-permute-done.refs_5_), channel_id=1, source_target_pairs={{0,4},{1,5},{2,6},{3,7},{4,0},{5,1},{6,2},{7,3},{8,12},{9,13},{10,... | collective-permute-start | bytes 5898248 | tf_op jit(solution)/shard_map/ppermute | solution.py:672
  895.9 4.3 collective-permute-start.12
  895.9 7.1 collective-permute-start.13

commit v3 on v2

--- a/solution.py
+++ b/solution.py
@@ -11,12 +11,12 @@
 MESH = pl.DeviceIdType.MESH
 LANES = 128
 VMEM = 67_000_000
-AHEAD = 4
+AHEAD = 8
 BUFFERS = 6
 LAG = 2
-SHARE_AT = 14
+SHARE_AT = 12
 RETIRE = 8
-WHOLE = 3
+WHOLE = 2
 WHOLE_AT = 2
 PARTS = 4
 GROUP = 2
@@ -60,7 +60,8 @@
 
 def gather_kernel(plan, q, k, v, o, g, u, d, h, slabs, own_0, own_1, whole, stop_0, stop_1, land_d, land_o, zbuf, tbuf,
                   z_recv, z_send, local, x_recv, y_recv, a_recv, b_recv, pair_recv, send, stop_recv, share_recv,
-                  share_send, land_recv, land_send, whole_recv, whole_send, whole_pair_recv, whole_pair_send):
+                  share_send, land_recv, land_send, whole_recv, whole_send, whole_pair_recv, whole_pair_send,
+                  keep_d, keep_o, keep_sem):
     z, dp = lax.axis_index("tp"), lax.axis_index("dp")
     core, x, y = dp % 2, (dp // 2) % 2, dp // 4
     x_peer = y * 4 + (1 - x) * 2 + core
@@ -288,50 +289,73 @@
 
 
     whole_columns = pl.ds(0, plan.whole)
+    keep = (keep_d, keep_o)
     mine = ((d, land_d, plan.down_rows, 0), (o, land_o, plan.out_rows, plan.downs))
     half = layers // 2
-
-    def whole_out():
-        for n, (source, land, _, _) in enumerate(mine):
-            for to, at in ((x_peer, 0), (y_peer, 2)):
-                target = land.at[my_rank]
-                remote(source.at[:, :, whole_columns], target, land_send.at[n], land_recv.at[at + n], dp=to)
-
-    def whole_forward():
-        for owner, at, first, to, then in ((x_peer, 0, half, y_peer, 6), (y_peer, 2, 0, x_peer, 4)):
-            for n, (_, land, _, _) in enumerate(mine):
-                wait_for(land.at[owner // 2], land_recv.at[at + n])
-                part = land.at[owner // 2, pl.ds(first, half)]
-                remote(part, part, land_send.at[n], land_recv.at[then + n], dp=to)
-
-    def whole_arrive():
-        for first, at in ((0, 4), (half, 6)):
-            for n, (_, land, _, _) in enumerate(mine):
-                wait_for(land.at[diagonal // 2, pl.ds(first, half)], land_recv.at[at + n])
 
     def whole_home(n, row):
         _, _, count, first = mine[n]
         return pl.ds(pl.multiple_of(first + row * count, 8), count)
 
-    def whole_to_rank(block, part):
-        flip_x, flip_y = block % 2, block // 2
-        rank = (y + flip_y * (1 - 2 * y)) * 2 + x + flip_x * (1 - 2 * x)
+    def landing(rank, some, act):
+        pl.when(rank == z)(lambda: act([whole.at[some, whole_home(n, core * plan.tp + z), :] for n in range(2)]))
+        pl.when(rank != z)(lambda: act([land.at[rank, some] for _, land, _, _ in mine]))
+
+    every = pl.ds(0, layers)
+
+    def whole_out():
+        def act(places):
+            for n, (source, _, _, _) in enumerate(mine):
+                for to, at in ((x_peer, 0), (y_peer, 2)):
+                    remote(source.at[:, :, whole_columns], places[n], land_send.at[n], land_recv.at[at + n], dp=to)
+
+        landing(my_rank, every, act)
+
+        @pl.when(stays)
+        def _():
+            for n, (source, _, _, _) in enumerate(mine):
+                pltpu.make_async_copy(source.at[:, :, whole_columns], keep[n], keep_sem.at[n]).start()
+
+    def whole_keep():
+        @pl.when(stays)
+        def _():
+            for n in range(2):
+                wait_for(keep[n], keep_sem.at[n])
+                target = whole.at[:, whole_home(n, core * plan.tp + z), :]
+                pltpu.make_async_copy(keep[n], target, keep_sem.at[2 + n]).start()
+
+    def whole_forward():
+        for owner, at, first, to, then in ((x_peer, 0, half, y_peer, 6), (y_peer, 2, 0, x_peer, 4)):
+            def arrived(places, at=at):
+                for n in range(2):
+                    wait_for(places[n], land_recv.at[at + n])
+
+            def on(places, to=to, then=then):
+                for n in range(2):
+                    remote(places[n], places[n], land_send.at[n], land_recv.at[then + n], dp=to)
+
+            landing(owner // 2, every, arrived)
+            landing(owner // 2, pl.ds(first, half), on)
+
+    def whole_arrive():
+        for first, at in ((0, 4), (half, 6)):
+            def arrived(places, at=at):
+                for n in range(2):
+                    wait_for(places[n], land_recv.at[at + n])
+
+            landing(diagonal // 2, pl.ds(first, half), arrived)
+
+    def whole_to_rank(shift, part):
+        rank = (z + shift + core * (plan.tp - 2 * shift)) % plan.tp
         some = pl.ds(part * (layers // PARTS), layers // PARTS)
 
         def move(sources):
             for n, source in enumerate(sources):
                 target = whole.at[some, whole_home(n, core * plan.tp + z), :]
-
-                @pl.when(rank != z)
-                def _(source=source, target=target, n=n):
-                    remote(source, target, whole_send.at[n], whole_recv.at[n], tp=rank)
-
-                @pl.when(rank == z)
-                def _(source=source, target=target, n=n):
-                    pltpu.make_async_copy(source, target, whole_recv.at[n]).start()
-
-        pl.when(block == 0)(lambda: move([source.at[some, :, whole_columns] for source, _, _, _ in mine]))
-        pl.when(block != 0)(lambda: move([land.at[rank, some] for _, land, _, _ in mine]))
+                remote(source, target, whole_send.at[n], whole_recv.at[n], tp=rank)
+
+        pl.when(rank == my_rank)(lambda: move([source.at[some, :, whole_columns] for source, _, _, _ in mine]))
+        pl.when(rank != my_rank)(lambda: move([land.at[rank, some] for _, land, _, _ in mine]))
 
     def whole_rows(which):
         return [
@@ -341,7 +365,13 @@
 
     def whole_to_pair():
         for n, part in enumerate(whole_rows(core)):
-            wait_for(part, whole_recv.at[n])
+            away = pl.ds(0, (plan.tp - 1) * mine[n][2])
+            wait_for(whole.at[:, away, :], whole_recv.at[n])
+
+            @pl.when(stays)
+            def _(n=n):
+                wait_for(keep[n], keep_sem.at[2 + n])
+
             remote(part, part, whole_pair_send.at[n], whole_pair_recv.at[n], dp=pair)
 
     def whole_finish():
@@ -389,15 +419,16 @@
 
         @pl.when(index == WHOLE_AT)
         def _():
+            whole_keep()
             whole_forward()
 
         @pl.when(index == WHOLE_AT + 3)
         def _():
             whole_arrive()
 
-        @pl.when((index >= WHOLE_AT) & (index < WHOLE_AT + 4 * PARTS))
-        def _():
-            whole_to_rank((index - WHOLE_AT) // PARTS, (index - WHOLE_AT) % PARTS)
+        @pl.when((index >= WHOLE_AT + 4) & (index < WHOLE_AT + 4 + (plan.tp - 1) * PARTS))
+        def _():
+            whole_to_rank((index - WHOLE_AT - 4) % (plan.tp - 1) + 1, (index - WHOLE_AT - 4) // (plan.tp - 1))
 
         @pl.when(index == ring - 2)
         def _():
@@ -473,6 +504,9 @@
             per_chunk, per_chunk, per_chunk, per_chunk, per_chunk, per_chunk,
             dma((2, plan.dp)), dma((2,)), dma((2,)),
             dma((8,)), dma((2,)), dma((2,)), dma((2,)), dma((2,)), dma((2,)),
+            pltpu.VMEM((plan.layers, plan.down_rows, plan.whole), jnp.bfloat16),
+            pltpu.VMEM((plan.layers, plan.out_rows, plan.whole), jnp.bfloat16),
+            dma((4,)),
         ],
         compiler_params=pltpu.CompilerParams(collective_id=0, has_side_effects=True),
         name="gather",

time: 907 us -> 826 us (0.911)
  Pallas kernels: 880 us -> 798 us
    pallas_call x1, Pallas kernels: 757 us -> 676 us  [gather(): pl.pallas_call(functools.partial(gather_kernel, plan), out_shape=[jax.Sha...]
  transfers between devices with their start and end apart: 14 -> 14, of which waited for: 7 -> 7; matrix products, arithmetic and copies ran while one was open for 0% -> 0% of each run, Pallas kernels for 13% -> 14%
where the time goes in v3:
time: 826 us
  Pallas kernels  798 us (97%)
  waiting for transfers between devices  19.2 us (2%)
    pallas_call x1, Pallas kernels, gather(): pl.pallas_call(functools.partial(gather_kernel, plan), out_shape=[jax.Sha...  676 us
    pallas_call x3, Pallas kernels, place_slabs(): pl.pallas_call(body, in_specs=[hbm] * (1 + len(held)), out_specs=[hbm] *...  91.6 us
    pallas_call x4, Pallas kernels, place_rows(): pl.pallas_call(body, out_shape=[outs[n] for n in made], in_specs=[hbm] *...  30.4 us
    ppermute x14, waiting for transfers between devices, swap(): return lax.ppermute(array, 'dp', [(i, i ^ bit) for i in range(plan.dp)])  19.2 us
  transfers between devices with their start and end apart: 14, of which 7 were waited for; matrix products, arithmetic and copies ran while one was open for 0% of the time, Pallas kernels for 14%

profile of v3, /device:TPU:0, one launch (start us, length us, event | category | flops | bytes accessed | tf_op | source)
XLA Modules:
  0.0 825.6 jit_solution(446955249070451113)
XLA Ops:
  0.6 676.2 %gather.1 = (bf16[8,32,2176,128]{3,2,1,0:T(8,128)(2,1)}, bf16[960,1024]{1,0:T(8,128)(2,1)}, bf16[960,1024]{1,0:T(8,128)(2,1)}, bf16[16,960,256]{2,1,0:T(8,128)(2...) custom-call(bf16[16,32,1024]{2,1,0:T(8,128)(2,1)} %q.1, ...), custom_call_target="tpu_custom_call" | custom-call | tf_op jit(solution)/shard_map/gather/pallas_call | solution.py:495
  676.9 1.4 collective-permute-start
  678.3 0.6 collective-permute-start.1
  678.9 1.4 collective-permute-start.4
  680.3 0.6 collective-permute-start.5
  681.0 45.5 %shard_map.119 = (bf16[16,768,1024]{2,1,0:T(8,128)(2,1)}, bf16[16,1408,1024]{2,1,0:T(8,128)(2,1)}) custom-call(bf16[8,32,2176,128]{3,2,1,0:T(8,128)(2,1)} %get-tuple-element.55.slab), custom_call_target="tpu_custom_call" | custom-call | flops 10000000 | bytes 142606336 | tf_op jit(solution)/shard_map/pallas_call | solution.py:566
  726.5 0.6 collective-permute-start.7
  727.1 33.8 %shard_map.120.refs_0_ = bf16[37984,1024]{1,0:T(8,128)(2,1)} custom-call(bf16[8,32,2176,128]{3,2,1,0:T(8,128)(2,1)} %get-tuple-element.55.slab), custom_call_target="tpu_custom_call" | custom-call | flops 10000000 | bytes 106954752 | tf_op jit(solution)/shard_map/pallas_call | solution.py:566
  760.9 3.4 collective-permute-done.4.refs_4_
  764.3 1.1 collective-permute-done.5.refs_9_
  765.4 0.5 collective-permute-start.8
  765.9 0.5 collective-permute-start.9
  766.4 0.6 collective-permute-start.2
  767.0 2.7 collective-permute-done.11.refs_11_
  769.7 0.6 collective-permute-start.3
  770.3 6.8 shard_map.121
  777.1 12.4 %shard_map.122.refs_14_ = bf16[37984,1024]{1,0:T(8,128)(2,1)} custom-call(bf16[8,32,2176,128]{3,2,1,0:T(8,128)(2,1)} %get-tuple-element.55.slab, bf16[37984,1024]{1,0:T(8,128)(2,1)} %shard_map.120.refs_0_), custom_call_target="tpu_custom_call", output_to_operand_aliasing={{}: (1, {})} | custom-call | flops 10000000 | bytes 35651584 | tf_op jit(solution)/shard_map/pallas_call | solution.py:566
  789.5 16.4 %shard_map.123 = (bf16[16,704,1024]{2,1,0:T(8,128)(2,1)}, bf16[16,1024,256]{2,1,0:T(8,128)(2,1)}, bf16[37984,1024]{1,0:T(8,128)(2,1)}) custom-call(bf16[960,1024]{1,0:T(8,128)(2,1)} %get-tuple-element.57.refs_0_, bf16[960,1024]{1,0:T(8,128)(2,1)} %get-tuple-element.58.refs_1_, ...), custom_call_target="tpu_custom_call", output_to_operand_aliasing={{0}: (12, {}), {1}: (13, {}), {2}: (14, {})} | custom-call | flops 10000000 | bytes 47185920 | tf_op jit(solution)/shard_map/pallas_call | solution.py:654
  805.8 5.7 collective-permute-done.2.refs_0_
  811.5 3.4 collective-permute-done.3.refs_1_
  814.9 0.5 collective-permute-start.13
  815.4 3.6 shard_map.124
  819.2 2.8 collective-permute-done.13.refs_1_
  822.0 3.6 shard_map.125
  (12 shorter events, 0.2 us)
Async XLA Ops:
  676.9 49.6 %collective-permute-start = (bf16[960,1024]{1,0:T(8,128)(2,1)}, bf16[960,1024]{1,0:T(8,128)(2,1)}, u32[]{:S(2)}, u32[]{:S(2)}) collective-permute-start(bf16[960,1024]{1,0:T(8,128)(2,1)} %get-tuple-element.58.refs_1_), channel_id=1, source_target_pairs={{0,2},{1,3},{2,0},{3,1},{4,6},{5,7},{6,4},{7,5},{8,10},{9,11},{10,... | collective-permute-start | bytes 5898248 | tf_op jit(solution)/shard_map/ppermute | solution.py:706
  678.3 48.8 %collective-permute-start.1 = (bf16[960,1024]{1,0:T(8,128)(2,1)}, bf16[960,1024]{1,0:T(8,128)(2,1)}, u32[]{:S(2)}, u32[]{:S(2)}) collective-permute-start(bf16[960,1024]{1,0:T(8,128)(2,1)} %get-tuple-element.57.refs_0_), channel_id=1, source_target_pairs={{0,4},{1,5},{2,6},{3,7},{4,0},{5,1},{6,2},{7,3},{8,12},{9,13},{10,... | collective-permute-start | bytes 5898248 | tf_op jit(solution)/shard_map/ppermute | solution.py:706
  678.9 85.3 %collective-permute-start.4 = (bf16[960,1024]{1,0:T(8,128)(2,1)}, bf16[960,1024]{1,0:T(8,128)(2,1)}, u32[]{:S(2)}, u32[]{:S(2)}) collective-permute-start(bf16[960,1024]{1,0:T(8,128)(2,1)} %get-tuple-element.57.refs_0_), channel_id=1, source_target_pairs={{0,2},{1,3},{2,0},{3,1},{4,6},{5,7},{6,4},{7,5},{8,10},{9,11},{10,... | collective-permute-start | bytes 5898248 | tf_op jit(solution)/shard_map/ppermute | solution.py:706
  680.3 85.0 %collective-permute-start.5 = (bf16[960,1024]{1,0:T(8,128)(2,1)}, bf16[960,1024]{1,0:T(8,128)(2,1)}, u32[]{:S(2)}, u32[]{:S(2)}) collective-permute-start(bf16[960,1024]{1,0:T(8,128)(2,1)} %get-tuple-element.58.refs_1_), channel_id=1, source_target_pairs={{0,4},{1,5},{2,6},{3,7},{4,0},{5,1},{6,2},{7,3},{8,12},{9,13},{10,... | collective-permute-start | bytes 5898248 | tf_op jit(solution)/shard_map/ppermute | solution.py:706
  681.0 84.9 %collective-permute-start.6 = (bf16[960,1024]{1,0:T(8,128)(2,1)}, bf16[960,1024]{1,0:T(8,128)(2,1)}, u32[]{:S(2)}, u32[]{:S(2)}) collective-permute-start(bf16[960,1024]{1,0:T(8,128)(2,1)} %get-tuple-element.57.refs_0_), channel_id=1, source_target_pairs={{0,1},{1,0},{2,3},{3,2},{4,5},{5,4},{6,7},{7,6},{8,9},{9,8},{10,11... | collective-permute-start | bytes 5898248 | tf_op jit(solution)/shard_map/ppermute | solution.py:706
  726.5 39.9 %collective-permute-start.7 = (bf16[960,1024]{1,0:T(8,128)(2,1)}, bf16[960,1024]{1,0:T(8,128)(2,1)}, u32[]{:S(2)}, u32[]{:S(2)}) collective-permute-start(bf16[960,1024]{1,0:T(8,128)(2,1)} %get-tuple-element.58.refs_1_), channel_id=1, source_target_pairs={{0,1},{1,0},{2,3},{3,2},{4,5},{5,4},{6,7},{7,6},{8,9},{9,8},{10,11... | collective-permute-start | bytes 5898248 | tf_op jit(solution)/shard_map/ppermute | solution.py:706
  765.4 4.3 collective-permute-start.11
  765.4 24.0 %collective-permute-start.8 = (bf16[960,1024]{1,0:T(8,128)(2,1)}, bf16[960,1024]{1,0:T(8,128)(2,1)}, u32[]{:S(2)}, u32[]{:S(2)}) collective-permute-start(bf16[960,1024]{1,0:T(8,128)(2,1)} %collective-permute-done.4.refs_4_), channel_id=1, source_target_pairs={{0,1},{1,0},{2,3},{3,2},{4,5},{5,4},{6,7},{7,6},{8,9},{9,8},{10,11... | collective-permute-start | bytes 5898248 | tf_op jit(solution)/shard_map/ppermute | solution.py:706
  765.9 23.5 %collective-permute-start.10 = (bf16[960,1024]{1,0:T(8,128)(2,1)}, bf16[960,1024]{1,0:T(8,128)(2,1)}, u32[]{:S(2)}, u32[]{:S(2)}) collective-permute-start(bf16[960,1024]{1,0:T(8,128)(2,1)} %collective-permute-done.1.refs_8_), channel_id=1, source_target_pairs={{0,1},{1,0},{2,3},{3,2},{4,5},{5,4},{6,7},{7,6},{8,9},{9,8},{10,11... | collective-permute-start | bytes 5898248 | tf_op jit(solution)/shard_map/ppermute | solution.py:706
  765.9 23.6 %collective-permute-start.9 = (bf16[960,1024]{1,0:T(8,128)(2,1)}, bf16[960,1024]{1,0:T(8,128)(2,1)}, u32[]{:S(2)}, u32[]{:S(2)}) collective-permute-start(bf16[960,1024]{1,0:T(8,128)(2,1)} %collective-permute-done.refs_5_), channel_id=1, source_target_pairs={{0,1},{1,0},{2,3},{3,2},{4,5},{5,4},{6,7},{7,6},{8,9},{9,8},{10,11... | collective-permute-start | bytes 5898248 | tf_op jit(solution)/shard_map/ppermute | solution.py:706
  766.4 45.1 %collective-permute-start.2 = (bf16[960,1024]{1,0:T(8,128)(2,1)}, bf16[960,1024]{1,0:T(8,128)(2,1)}, u32[]{:S(2)}, u32[]{:S(2)}) collective-permute-start(bf16[960,1024]{1,0:T(8,128)(2,1)} %collective-permute-done.1.refs_8_), channel_id=1, source_target_pairs={{0,2},{1,3},{2,0},{3,1},{4,6},{5,7},{6,4},{7,5},{8,10},{9,11},{10,... | collective-permute-start | bytes 5898248 | tf_op jit(solution)/shard_map/ppermute | solution.py:706
  769.7 45.2 %collective-permute-start.3 = (bf16[960,1024]{1,0:T(8,128)(2,1)}, bf16[960,1024]{1,0:T(8,128)(2,1)}, u32[]{:S(2)}, u32[]{:S(2)}) collective-permute-start(bf16[960,1024]{1,0:T(8,128)(2,1)} %collective-permute-done.refs_5_), channel_id=1, source_target_pairs={{0,4},{1,5},{2,6},{3,7},{4,0},{5,1},{6,2},{7,3},{8,12},{9,13},{10,... | collective-permute-start | bytes 5898248 | tf_op jit(solution)/shard_map/ppermute | solution.py:706
  814.9 4.3 collective-permute-start.12
  814.9 7.1 collective-permute-start.13

commit v4 on v3

--- a/solution.py
+++ b/solution.py
@@ -11,15 +11,16 @@
 MESH = pl.DeviceIdType.MESH
 LANES = 128
 VMEM = 67_000_000
-AHEAD = 8
+AHEAD = 14
 BUFFERS = 6
 LAG = 2
-SHARE_AT = 12
+SHARE_AT = 20
 RETIRE = 8
-WHOLE = 2
+WHOLE = 3
 WHOLE_AT = 2
+RANKS_AT = 10
 PARTS = 4
-GROUP = 2
+GROUP = 4
 
 
 class Plan:
@@ -413,9 +414,9 @@
         def _():
             start_exchange(index + AHEAD)
 
-        @pl.when((index >= SHARE_AT) & (index < SHARE_AT + 2 * plan.dp) & (index % 2 == SHARE_AT % 2))
-        def _():
-            share_to_rank((index - SHARE_AT) // 2)
+        @pl.when((index >= SHARE_AT) & (index < SHARE_AT + plan.dp))
+        def _():
+            share_to_rank(index - SHARE_AT)
 
         @pl.when(index == WHOLE_AT)
         def _():
@@ -426,9 +427,9 @@
         def _():
             whole_arrive()
 
-        @pl.when((index >= WHOLE_AT + 4) & (index < WHOLE_AT + 4 + (plan.tp - 1) * PARTS))
-        def _():
-            whole_to_rank((index - WHOLE_AT - 4) % (plan.tp - 1) + 1, (index - WHOLE_AT - 4) // (plan.tp - 1))
+        @pl.when((index >= RANKS_AT) & (index < RANKS_AT + (plan.tp - 1) * PARTS))
+        def _():
+            whole_to_rank((index - RANKS_AT) % (plan.tp - 1) + 1, (index - RANKS_AT) // (plan.tp - 1))
 
         @pl.when(index == ring - 2)
         def _():

time: 826 us -> 791 us (0.958)
  Pallas kernels: 798 us -> 765 us
    pallas_call x1, Pallas kernels: 676 us -> 642 us  [gather(): pl.pallas_call(functools.partial(gather_kernel, plan), out_shape=[jax.Sha...]
  transfers between devices with their start and end apart: 14 -> 14, of which waited for: 7 -> 7; matrix products, arithmetic and copies ran while one was open for 0% -> 0% of each run, Pallas kernels for 14% -> 15%
where the time goes in v4:
time: 791 us
  Pallas kernels  765 us (97%)
  waiting for transfers between devices  17.9 us (2%)
    pallas_call x1, Pallas kernels, gather(): pl.pallas_call(functools.partial(gather_kernel, plan), out_shape=[jax.Sha...  642 us
    pallas_call x3, Pallas kernels, place_slabs(): pl.pallas_call(body, in_specs=[hbm] * (1 + len(held)), out_specs=[hbm] *...  89.8 us
    pallas_call x4, Pallas kernels, place_rows(): pl.pallas_call(body, out_shape=[outs[n] for n in made], in_specs=[hbm] *...  33.4 us
    ppermute x14, waiting for transfers between devices, swap(): return lax.ppermute(array, 'dp', [(i, i ^ bit) for i in range(plan.dp)])  17.9 us
  transfers between devices with their start and end apart: 14, of which 7 were waited for; matrix products, arithmetic and copies ran while one was open for 0% of the time, Pallas kernels for 15%

profile of v4, /device:TPU:0, one launch (start us, length us, event | category | flops | bytes accessed | tf_op | source)
XLA Modules:
  0.0 791.3 jit_solution(702380582690265481)
XLA Ops:
  0.6 641.9 %gather.1 = (bf16[8,31,2176,128]{3,2,1,0:T(8,128)(2,1)}, bf16[960,1024]{1,0:T(8,128)(2,1)}, bf16[960,1024]{1,0:T(8,128)(2,1)}, bf16[16,960,384]{2,1,0:T(8,128)(2...) custom-call(bf16[16,32,1024]{2,1,0:T(8,128)(2,1)} %q.1, ...), custom_call_target="tpu_custom_call" | custom-call | tf_op jit(solution)/shard_map/gather/pallas_call | solution.py:496
  642.6 1.4 collective-permute-start
  644.0 0.6 collective-permute-start.1
  644.6 1.3 collective-permute-start.4
  646.0 0.7 collective-permute-start.5
  646.7 45.5 %shard_map.119 = (bf16[16,768,1024]{2,1,0:T(8,128)(2,1)}, bf16[16,1408,1024]{2,1,0:T(8,128)(2,1)}) custom-call(bf16[8,31,2176,128]{3,2,1,0:T(8,128)(2,1)} %get-tuple-element.55.slab), custom_call_target="tpu_custom_call" | custom-call | flops 10000000 | bytes 142606336 | tf_op jit(solution)/shard_map/pallas_call | solution.py:567
  692.2 0.6 collective-permute-start.7
  692.7 34.0 %shard_map.120.refs_0_ = bf16[37984,1024]{1,0:T(8,128)(2,1)} custom-call(bf16[8,31,2176,128]{3,2,1,0:T(8,128)(2,1)} %get-tuple-element.55.slab), custom_call_target="tpu_custom_call" | custom-call | flops 10000000 | bytes 106954752 | tf_op jit(solution)/shard_map/pallas_call | solution.py:567
  726.7 3.2 collective-permute-done.4.refs_4_
  729.9 1.1 collective-permute-done.5.refs_9_
  731.0 0.5 collective-permute-start.8
  731.6 0.5 collective-permute-start.9
  732.1 0.6 collective-permute-start.2
  732.7 2.6 collective-permute-done.11.refs_11_
  735.4 0.6 collective-permute-start.3
  736.0 9.4 %shard_map.121 = (bf16[16,704,1024]{2,1,0:T(8,128)(2,1)}, bf16[16,1024,256]{2,1,0:T(8,128)(2,1)}) custom-call(bf16[16,960,384]{2,1,0:T(8,128)(2,1)} %get-tuple-element.52.refs_0_), custom_call_target="tpu_custom_call" | custom-call | flops 10000000 | bytes 23592960 | tf_op jit(solution)/shard_map/pallas_call | solution.py:655
  745.4 10.4 %shard_map.122.refs_14_ = bf16[37984,1024]{1,0:T(8,128)(2,1)} custom-call(bf16[8,31,2176,128]{3,2,1,0:T(8,128)(2,1)} %get-tuple-element.55.slab, bf16[37984,1024]{1,0:T(8,128)(2,1)} %shard_map.120.refs_0_), custom_call_target="tpu_custom_call", output_to_operand_aliasing={{}: (1, {})} | custom-call | flops 10000000 | bytes 26738688 | tf_op jit(solution)/shard_map/pallas_call | solution.py:567
  755.8 16.8 %shard_map.123 = (bf16[16,704,1024]{2,1,0:T(8,128)(2,1)}, bf16[16,1024,256]{2,1,0:T(8,128)(2,1)}, bf16[37984,1024]{1,0:T(8,128)(2,1)}) custom-call(bf16[960,1024]{1,0:T(8,128)(2,1)} %get-tuple-element.57.refs_0_, bf16[960,1024]{1,0:T(8,128)(2,1)} %get-tuple-element.58.refs_1_, ...), custom_call_target="tpu_custom_call", output_to_operand_aliasing={{0}: (12, {}), {1}: (13, {}), {2}: (14, {})} | custom-call | flops 10000000 | bytes 47185920 | tf_op jit(solution)/shard_map/pallas_call | solution.py:655
  772.6 4.6 collective-permute-done.2.refs_0_
  777.2 3.4 collective-permute-done.3.refs_1_
  780.5 0.5 collective-permute-start.13
  781.0 3.6 shard_map.124
  784.9 2.8 collective-permute-done.13.refs_1_
  787.7 3.6 shard_map.125
  (12 shorter events, 0.2 us)
Async XLA Ops:
  642.6 49.6 %collective-permute-start = (bf16[960,1024]{1,0:T(8,128)(2,1)}, bf16[960,1024]{1,0:T(8,128)(2,1)}, u32[]{:S(2)}, u32[]{:S(2)}) collective-permute-start(bf16[960,1024]{1,0:T(8,128)(2,1)} %get-tuple-element.58.refs_1_), channel_id=1, source_target_pairs={{0,2},{1,3},{2,0},{3,1},{4,6},{5,7},{6,4},{7,5},{8,10},{9,11},{10,... | collective-permute-start | bytes 5898248 | tf_op jit(solution)/shard_map/ppermute | solution.py:707
  644.0 48.7 %collective-permute-start.1 = (bf16[960,1024]{1,0:T(8,128)(2,1)}, bf16[960,1024]{1,0:T(8,128)(2,1)}, u32[]{:S(2)}, u32[]{:S(2)}) collective-permute-start(bf16[960,1024]{1,0:T(8,128)(2,1)} %get-tuple-element.57.refs_0_), channel_id=1, source_target_pairs={{0,4},{1,5},{2,6},{3,7},{4,0},{5,1},{6,2},{7,3},{8,12},{9,13},{10,... | collective-permute-start | bytes 5898248 | tf_op jit(solution)/shard_map/ppermute | solution.py:707
  644.6 85.3 %collective-permute-start.4 = (bf16[960,1024]{1,0:T(8,128)(2,1)}, bf16[960,1024]{1,0:T(8,128)(2,1)}, u32[]{:S(2)}, u32[]{:S(2)}) collective-permute-start(bf16[960,1024]{1,0:T(8,128)(2,1)} %get-tuple-element.57.refs_0_), channel_id=1, source_target_pairs={{0,2},{1,3},{2,0},{3,1},{4,6},{5,7},{6,4},{7,5},{8,10},{9,11},{10,... | collective-permute-start | bytes 5898248 | tf_op jit(solution)/shard_map/ppermute | solution.py:707
  646.0 85.0 %collective-permute-start.5 = (bf16[960,1024]{1,0:T(8,128)(2,1)}, bf16[960,1024]{1,0:T(8,128)(2,1)}, u32[]{:S(2)}, u32[]{:S(2)}) collective-permute-start(bf16[960,1024]{1,0:T(8,128)(2,1)} %get-tuple-element.58.refs_1_), channel_id=1, source_target_pairs={{0,4},{1,5},{2,6},{3,7},{4,0},{5,1},{6,2},{7,3},{8,12},{9,13},{10,... | collective-permute-start | bytes 5898248 | tf_op jit(solution)/shard_map/ppermute | solution.py:707
  646.7 84.9 %collective-permute-start.6 = (bf16[960,1024]{1,0:T(8,128)(2,1)}, bf16[960,1024]{1,0:T(8,128)(2,1)}, u32[]{:S(2)}, u32[]{:S(2)}) collective-permute-start(bf16[960,1024]{1,0:T(8,128)(2,1)} %get-tuple-element.57.refs_0_), channel_id=1, source_target_pairs={{0,1},{1,0},{2,3},{3,2},{4,5},{5,4},{6,7},{7,6},{8,9},{9,8},{10,11... | collective-permute-start | bytes 5898248 | tf_op jit(solution)/shard_map/ppermute | solution.py:707
  692.2 39.9 %collective-permute-start.7 = (bf16[960,1024]{1,0:T(8,128)(2,1)}, bf16[960,1024]{1,0:T(8,128)(2,1)}, u32[]{:S(2)}, u32[]{:S(2)}) collective-permute-start(bf16[960,1024]{1,0:T(8,128)(2,1)} %get-tuple-element.58.refs_1_), channel_id=1, source_target_pairs={{0,1},{1,0},{2,3},{3,2},{4,5},{5,4},{6,7},{7,6},{8,9},{9,8},{10,11... | collective-permute-start | bytes 5898248 | tf_op jit(solution)/shard_map/ppermute | solution.py:707
  731.0 4.3 collective-permute-start.11
  731.0 24.8 %collective-permute-start.8 = (bf16[960,1024]{1,0:T(8,128)(2,1)}, bf16[960,1024]{1,0:T(8,128)(2,1)}, u32[]{:S(2)}, u32[]{:S(2)}) collective-permute-start(bf16[960,1024]{1,0:T(8,128)(2,1)} %collective-permute-done.4.refs_4_), channel_id=1, source_target_pairs={{0,1},{1,0},{2,3},{3,2},{4,5},{5,4},{6,7},{7,6},{8,9},{9,8},{10,11... | collective-permute-start | bytes 5898248 | tf_op jit(solution)/shard_map/ppermute | solution.py:707
  731.6 24.3 %collective-permute-start.10 = (bf16[960,1024]{1,0:T(8,128)(2,1)}, bf16[960,1024]{1,0:T(8,128)(2,1)}, u32[]{:S(2)}, u32[]{:S(2)}) collective-permute-start(bf16[960,1024]{1,0:T(8,128)(2,1)} %collective-permute-done.1.refs_8_), channel_id=1, source_target_pairs={{0,1},{1,0},{2,3},{3,2},{4,5},{5,4},{6,7},{7,6},{8,9},{9,8},{10,11... | collective-permute-start | bytes 5898248 | tf_op jit(solution)/shard_map/ppermute | solution.py:707
  731.6 24.3 %collective-permute-start.9 = (bf16[960,1024]{1,0:T(8,128)(2,1)}, bf16[960,1024]{1,0:T(8,128)(2,1)}, u32[]{:S(2)}, u32[]{:S(2)}) collective-permute-start(bf16[960,1024]{1,0:T(8,128)(2,1)} %collective-permute-done.refs_5_), channel_id=1, source_target_pairs={{0,1},{1,0},{2,3},{3,2},{4,5},{5,4},{6,7},{7,6},{8,9},{9,8},{10,11... | collective-permute-start | bytes 5898248 | tf_op jit(solution)/shard_map/ppermute | solution.py:707
  732.1 45.1 %collective-permute-start.2 = (bf16[960,1024]{1,0:T(8,128)(2,1)}, bf16[960,1024]{1,0:T(8,128)(2,1)}, u32[]{:S(2)}, u32[]{:S(2)}) collective-permute-start(bf16[960,1024]{1,0:T(8,128)(2,1)} %collective-permute-done.1.refs_8_), channel_id=1, source_target_pairs={{0,2},{1,3},{2,0},{3,1},{4,6},{5,7},{6,4},{7,5},{8,10},{9,11},{10,... | collective-permute-start | bytes 5898248 | tf_op jit(solution)/shard_map/ppermute | solution.py:707
  735.4 45.2 %collective-permute-start.3 = (bf16[960,1024]{1,0:T(8,128)(2,1)}, bf16[960,1024]{1,0:T(8,128)(2,1)}, u32[]{:S(2)}, u32[]{:S(2)}) collective-permute-start(bf16[960,1024]{1,0:T(8,128)(2,1)} %collective-permute-done.refs_5_), channel_id=1, source_target_pairs={{0,4},{1,5},{2,6},{3,7},{4,0},{5,1},{6,2},{7,3},{8,12},{9,13},{10,... | collective-permute-start | bytes 5898248 | tf_op jit(solution)/shard_map/ppermute | solution.py:707
  780.5 4.3 collective-permute-start.12
  780.5 7.1 collective-permute-start.13

commit v5 on v4

--- a/solution.py
+++ b/solution.py
@@ -62,7 +62,7 @@
 def gather_kernel(plan, q, k, v, o, g, u, d, h, slabs, own_0, own_1, whole, stop_0, stop_1, land_d, land_o, zbuf, tbuf,
                   z_recv, z_send, local, x_recv, y_recv, a_recv, b_recv, pair_recv, send, stop_recv, share_recv,
                   share_send, land_recv, land_send, whole_recv, whole_send, whole_pair_recv, whole_pair_send,
-                  keep_d, keep_o, keep_sem):
+                  keep_d, keep_o, keep_sem, packed, pack_sem):
     z, dp = lax.axis_index("tp"), lax.axis_index("dp")
     core, x, y = dp % 2, (dp // 2) % 2, dp // 4
     x_peer = y * 4 + (1 - x) * 2 + core
@@ -83,50 +83,54 @@
         pltpu.make_async_copy(ref, ref, sem).wait()
 
 
-    def exchange(pieces, chunks, index):
+    def rank_at(step):
+        return (z + step + core * (plan.tp - 2 * step)) % plan.tp
+
+    def layer_pieces(first, rank):
+        some, part, wide = pl.ds(first, GROUP), plan.part, plan.wide_window
+        narrow = lanes(rank * (part // LANES), part)
+        window = lanes(plan.wide_base(rank), wide)
+        return [
+            (q.at[some, :, narrow], 0, part),
+            (k.at[some, :, narrow], part, part),
+            (v.at[some, :, narrow], 2 * part, part),
+            (g.at[some, :, window], 3 * part, wide),
+            (u.at[some, :, window], 3 * part + wide, wide),
+        ]
+
+    def collect(group):
         for step in range(1, plan.tp):
-            rank = (z + step + core * (plan.tp - 2 * step)) % plan.tp
-            for source, column, width in pieces(rank):
-                target = zbuf.at[chunks, my_rows, pl.ds(column, width)]
-                remote(source, target, z_send.at[index], z_recv.at[index], tp=rank)
-        for source, column, width in pieces(z):
-            target = zbuf.at[chunks, my_rows, pl.ds(column, width)]
-            pltpu.make_async_copy(source, target, z_recv.at[index]).start()
-
-    def layer_pieces(some):
-        def pieces(rank):
-            part, wide = plan.part, plan.wide_window
-            narrow = lanes(rank * (part // LANES), part)
-            window = lanes(plan.wide_base(rank), wide)
-            return [
-                (q.at[some, :, narrow], 0, part),
-                (k.at[some, :, narrow], part, part),
-                (v.at[some, :, narrow], 2 * part, part),
-                (g.at[some, :, window], 3 * part, wide),
-                (u.at[some, :, window], 3 * part + wide, wide),
-            ]
-
-        return pieces
-
-    def head_pieces(step, width):
-        def pieces(rank):
-            return [(h.at[:, lanes(plan.head_base(rank) + step * (chunk // LANES), width)], 0, width)]
-
-        return pieces
+            for source, column, width in layer_pieces(group * GROUP, rank_at(step)):
+                target = packed.at[group, step - 1, :, :, pl.ds(column, width)]
+                pltpu.make_async_copy(source, target, pack_sem.at[group]).start()
+        for source, column, width in layer_pieces(group * GROUP, z):
+            target = zbuf.at[pl.ds(group * GROUP, GROUP), my_rows, pl.ds(column, width)]
+            pltpu.make_async_copy(source, target, z_recv.at[group * GROUP]).start()
+
+    def exchange_layers(group):
+        wait_for(packed.at[group], pack_sem.at[group])
+        for step in range(1, plan.tp):
+            index = group * GROUP
+            target = zbuf.at[pl.ds(index, GROUP), my_rows, :]
+            remote(packed.at[group, step - 1], target, z_send.at[index], z_recv.at[index], tp=rank_at(step))
+
+    def exchange_head(index, width):
+        def piece(rank):
+            return h.at[:, lanes(plan.head_base(rank) + (index - layers) * (chunk // LANES), width)]
+
+        target = zbuf.at[index, my_rows, pl.ds(0, width)]
+        for step in range(1, plan.tp):
+            remote(piece(rank_at(step)), target, z_send.at[index], z_recv.at[index], tp=rank_at(step))
+        pltpu.make_async_copy(piece(z), target, z_recv.at[index]).start()
 
     def start_exchange(index):
-        @pl.when((index < layers) & (index % GROUP == 0))
-        def _():
-            some = pl.ds(index, GROUP)
-            exchange(layer_pieces(some), some, index)
-
         @pl.when((index >= layers) & (index < last))
         def _():
-            exchange(head_pieces(index - layers, chunk), index, index)
+            exchange_head(index, chunk)
 
         @pl.when(index == last)
         def _():
-            exchange(head_pieces(last - layers, plan.tail_window), last, last)
+            exchange_head(last, plan.tail_window)
 
     def wait_exchange(index, width):
         wait_for(zbuf.at[index, :, pl.ds(0, width)], z_recv.at[index])
@@ -382,17 +386,22 @@
             wait_for(whole_rows(core)[n], whole_pair_send.at[n])
             wait_for(whole_rows(1 - core)[n], whole_pair_recv.at[n])
 
+    groups = layers // GROUP
     barrier = pltpu.get_barrier_semaphore()
     peers = [{"tp": (z + step) % plan.tp} for step in range(1, plan.tp)]
     peers += [{"dp": (dp + step) % plan.dp} for step in range(1, plan.dp)]
     for peer in peers:
         pl.semaphore_signal(barrier, inc=1, device_id=peer, device_id_type=MESH)
+    for group in range(groups):
+        collect(group)
     pl.semaphore_wait(barrier, len(peers))
 
-    start_exchange(0)
     whole_out()
+    exchange_layers(0)
     share_in_plane()
-    for index in range(GROUP, AHEAD):
+    for group in range(1, groups):
+        exchange_layers(group)
+    for index in range(layers, AHEAD):
         start_exchange(index)
 
     def retire(index):
@@ -430,10 +439,6 @@
         @pl.when((index >= RANKS_AT) & (index < RANKS_AT + (plan.tp - 1) * PARTS))
         def _():
             whole_to_rank((index - RANKS_AT) % (plan.tp - 1) + 1, (index - RANKS_AT) // (plan.tp - 1))
-
-        @pl.when(index == ring - 2)
-        def _():
-            whole_to_pair()
 
         @pl.when(index < layers)
         def _():
@@ -466,6 +471,8 @@
     make_extra()
     for index in range(ring - LAG, ring):
         forward(slab_view(index), index, chunk)
+        if index == ring - LAG:
+            whole_to_pair()
     forward(slab_view(ring), ring, tail)
     for index in range(ring - 2 * LAG, ring):
         forward_diagonal(slab_view(index), index, chunk)
@@ -508,6 +515,8 @@
             pltpu.VMEM((plan.layers, plan.down_rows, plan.whole), jnp.bfloat16),
             pltpu.VMEM((plan.layers, plan.out_rows, plan.whole), jnp.bfloat16),
             dma((4,)),
+            pltpu.VMEM((plan.layers // GROUP, plan.tp - 1, GROUP, plan.rows, plan.layer_window), jnp.bfloat16),
+            dma((plan.layers // GROUP,)),
         ],
         compiler_params=pltpu.CompilerParams(collective_id=0, has_side_effects=True),
         name="gather",

time: 791 us -> 788 us (level)
  no operation moved by 1% of the time
where the time goes in v5:
time: 788 us
  Pallas kernels  760 us (96%)
  waiting for transfers between devices  19.2 us (2%)
    pallas_call x1, Pallas kernels, gather(): pl.pallas_call(functools.partial(gather_kernel, plan), out_shape=[jax.Sha...  637 us
    pallas_call x3, Pallas kernels, place_slabs(): pl.pallas_call(body, in_specs=[hbm] * (1 + len(held)), out_specs=[hbm] *...  89.8 us
    pallas_call x4, Pallas kernels, place_rows(): pl.pallas_call(body, out_shape=[outs[n] for n in made], in_specs=[hbm] *...  33.4 us
    ppermute x14, waiting for transfers between devices, swap(): return lax.ppermute(array, 'dp', [(i, i ^ bit) for i in range(plan.dp)])  19.2 us
  transfers between devices with their start and end apart: 14, of which 7 were waited for; matrix products, arithmetic and copies ran while one was open for 0% of the time, Pallas kernels for 15%

profile of v5, /device:TPU:0, one launch (start us, length us, event | category | flops | bytes accessed | tf_op | source)
XLA Modules:
  0.0 787.6 jit_solution(9190199498428019321)
XLA Ops:
  0.6 637.2 %gather.1 = (bf16[8,31,2176,128]{3,2,1,0:T(8,128)(2,1)}, bf16[960,1024]{1,0:T(8,128)(2,1)}, bf16[960,1024]{1,0:T(8,128)(2,1)}, bf16[16,960,384]{2,1,0:T(8,128)(2...) custom-call(bf16[16,32,1024]{2,1,0:T(8,128)(2,1)} %q.1, ...), custom_call_target="tpu_custom_call" | custom-call | tf_op jit(solution)/shard_map/gather/pallas_call | solution.py:503
  637.8 2.3 collective-permute-start
  640.2 1.9 collective-permute-start.4
  642.1 0.1 collective-permute-start.5
  642.3 45.5 %shard_map.119 = (bf16[16,768,1024]{2,1,0:T(8,128)(2,1)}, bf16[16,1408,1024]{2,1,0:T(8,128)(2,1)}) custom-call(bf16[8,31,2176,128]{3,2,1,0:T(8,128)(2,1)} %get-tuple-element.55.slab), custom_call_target="tpu_custom_call" | custom-call | flops 10000000 | bytes 142606336 | tf_op jit(solution)/shard_map/pallas_call | solution.py:576
  687.7 0.6 collective-permute-start.7
  688.3 34.0 %shard_map.120.refs_0_ = bf16[37984,1024]{1,0:T(8,128)(2,1)} custom-call(bf16[8,31,2176,128]{3,2,1,0:T(8,128)(2,1)} %get-tuple-element.55.slab), custom_call_target="tpu_custom_call" | custom-call | flops 10000000 | bytes 106954752 | tf_op jit(solution)/shard_map/pallas_call | solution.py:576
  722.3 3.6 collective-permute-done.4.refs_4_
  725.9 1.5 collective-permute-done.5.refs_9_
  727.3 0.5 collective-permute-start.8
  727.8 0.5 collective-permute-start.9
  728.4 0.4 collective-permute-start.2
  728.7 2.9 collective-permute-done.11.refs_11_
  731.6 0.3 collective-permute-start.3
  732.0 9.4 %shard_map.121 = (bf16[16,704,1024]{2,1,0:T(8,128)(2,1)}, bf16[16,1024,256]{2,1,0:T(8,128)(2,1)}) custom-call(bf16[16,960,384]{2,1,0:T(8,128)(2,1)} %get-tuple-element.52.refs_0_), custom_call_target="tpu_custom_call" | custom-call | flops 10000000 | bytes 23592960 | tf_op jit(solution)/shard_map/pallas_call | solution.py:664
  741.4 10.4 %shard_map.122.refs_14_ = bf16[37984,1024]{1,0:T(8,128)(2,1)} custom-call(bf16[8,31,2176,128]{3,2,1,0:T(8,128)(2,1)} %get-tuple-element.55.slab, bf16[37984,1024]{1,0:T(8,128)(2,1)} %shard_map.120.refs_0_), custom_call_target="tpu_custom_call", output_to_operand_aliasing={{}: (1, {})} | custom-call | flops 10000000 | bytes 26738688 | tf_op jit(solution)/shard_map/pallas_call | solution.py:576
  751.8 16.8 %shard_map.123 = (bf16[16,704,1024]{2,1,0:T(8,128)(2,1)}, bf16[16,1024,256]{2,1,0:T(8,128)(2,1)}, bf16[37984,1024]{1,0:T(8,128)(2,1)}) custom-call(bf16[960,1024]{1,0:T(8,128)(2,1)} %get-tuple-element.57.refs_0_, bf16[960,1024]{1,0:T(8,128)(2,1)} %get-tuple-element.58.refs_1_, ...), custom_call_target="tpu_custom_call", output_to_operand_aliasing={{0}: (12, {}), {1}: (13, {}), {2}: (14, {})} | custom-call | flops 10000000 | bytes 47185920 | tf_op jit(solution)/shard_map/pallas_call | solution.py:664
  768.6 4.9 collective-permute-done.2.refs_0_
  773.5 3.4 collective-permute-done.3.refs_1_
  776.8 0.5 collective-permute-start.13
  777.3 3.6 shard_map.124
  781.0 0.2 collective-permute-done.12.refs_0_
  781.1 2.8 collective-permute-done.13.refs_1_
  783.9 3.6 shard_map.125
  (12 shorter events, 0.1 us)
Async XLA Ops:
  637.8 49.9 %collective-permute-start = (bf16[960,1024]{1,0:T(8,128)(2,1)}, bf16[960,1024]{1,0:T(8,128)(2,1)}, u32[]{:S(2)}, u32[]{:S(2)}) collective-permute-start(bf16[960,1024]{1,0:T(8,128)(2,1)} %get-tuple-element.58.refs_1_), channel_id=1, source_target_pairs={{0,2},{1,3},{2,0},{3,1},{4,6},{5,7},{6,4},{7,5},{8,10},{9,11},{10,... | collective-permute-start | bytes 5898248 | tf_op jit(solution)/shard_map/ppermute | solution.py:716
  640.2 48.2 %collective-permute-start.1 = (bf16[960,1024]{1,0:T(8,128)(2,1)}, bf16[960,1024]{1,0:T(8,128)(2,1)}, u32[]{:S(2)}, u32[]{:S(2)}) collective-permute-start(bf16[960,1024]{1,0:T(8,128)(2,1)} %get-tuple-element.57.refs_0_), channel_id=1, source_target_pairs={{0,4},{1,5},{2,6},{3,7},{4,0},{5,1},{6,2},{7,3},{8,12},{9,13},{10,... | collective-permute-start | bytes 5898248 | tf_op jit(solution)/shard_map/ppermute | solution.py:716
  640.2 85.7 %collective-permute-start.4 = (bf16[960,1024]{1,0:T(8,128)(2,1)}, bf16[960,1024]{1,0:T(8,128)(2,1)}, u32[]{:S(2)}, u32[]{:S(2)}) collective-permute-start(bf16[960,1024]{1,0:T(8,128)(2,1)} %get-tuple-element.57.refs_0_), channel_id=1, source_target_pairs={{0,2},{1,3},{2,0},{3,1},{4,6},{5,7},{6,4},{7,5},{8,10},{9,11},{10,... | collective-permute-start | bytes 5898248 | tf_op jit(solution)/shard_map/ppermute | solution.py:716
  642.1 85.2 %collective-permute-start.5 = (bf16[960,1024]{1,0:T(8,128)(2,1)}, bf16[960,1024]{1,0:T(8,128)(2,1)}, u32[]{:S(2)}, u32[]{:S(2)}) collective-permute-start(bf16[960,1024]{1,0:T(8,128)(2,1)} %get-tuple-element.58.refs_1_), channel_id=1, source_target_pairs={{0,4},{1,5},{2,6},{3,7},{4,0},{5,1},{6,2},{7,3},{8,12},{9,13},{10,... | collective-permute-start | bytes 5898248 | tf_op jit(solution)/shard_map/ppermute | solution.py:716
  642.3 85.6 %collective-permute-start.6 = (bf16[960,1024]{1,0:T(8,128)(2,1)}, bf16[960,1024]{1,0:T(8,128)(2,1)}, u32[]{:S(2)}, u32[]{:S(2)}) collective-permute-start(bf16[960,1024]{1,0:T(8,128)(2,1)} %get-tuple-element.57.refs_0_), channel_id=1, source_target_pairs={{0,1},{1,0},{2,3},{3,2},{4,5},{5,4},{6,7},{7,6},{8,9},{9,8},{10,11... | collective-permute-start | bytes 5898248 | tf_op jit(solution)/shard_map/ppermute | solution.py:716
  687.7 40.6 %collective-permute-start.7 = (bf16[960,1024]{1,0:T(8,128)(2,1)}, bf16[960,1024]{1,0:T(8,128)(2,1)}, u32[]{:S(2)}, u32[]{:S(2)}) collective-permute-start(bf16[960,1024]{1,0:T(8,128)(2,1)} %get-tuple-element.58.refs_1_), channel_id=1, source_target_pairs={{0,1},{1,0},{2,3},{3,2},{4,5},{5,4},{6,7},{7,6},{8,9},{9,8},{10,11... | collective-permute-start | bytes 5898248 | tf_op jit(solution)/shard_map/ppermute | solution.py:716
  727.3 4.3 collective-permute-start.11
  727.3 24.4 %collective-permute-start.8 = (bf16[960,1024]{1,0:T(8,128)(2,1)}, bf16[960,1024]{1,0:T(8,128)(2,1)}, u32[]{:S(2)}, u32[]{:S(2)}) collective-permute-start(bf16[960,1024]{1,0:T(8,128)(2,1)} %collective-permute-done.4.refs_4_), channel_id=1, source_target_pairs={{0,1},{1,0},{2,3},{3,2},{4,5},{5,4},{6,7},{7,6},{8,9},{9,8},{10,11... | collective-permute-start | bytes 5898248 | tf_op jit(solution)/shard_map/ppermute | solution.py:716
  727.8 23.9 %collective-permute-start.10 = (bf16[960,1024]{1,0:T(8,128)(2,1)}, bf16[960,1024]{1,0:T(8,128)(2,1)}, u32[]{:S(2)}, u32[]{:S(2)}) collective-permute-start(bf16[960,1024]{1,0:T(8,128)(2,1)} %collective-permute-done.1.refs_8_), channel_id=1, source_target_pairs={{0,1},{1,0},{2,3},{3,2},{4,5},{5,4},{6,7},{7,6},{8,9},{9,8},{10,11... | collective-permute-start | bytes 5898248 | tf_op jit(solution)/shard_map/ppermute | solution.py:716
  727.8 23.9 %collective-permute-start.9 = (bf16[960,1024]{1,0:T(8,128)(2,1)}, bf16[960,1024]{1,0:T(8,128)(2,1)}, u32[]{:S(2)}, u32[]{:S(2)}) collective-permute-start(bf16[960,1024]{1,0:T(8,128)(2,1)} %collective-permute-done.refs_5_), channel_id=1, source_target_pairs={{0,1},{1,0},{2,3},{3,2},{4,5},{5,4},{6,7},{7,6},{8,9},{9,8},{10,11... | collective-permute-start | bytes 5898248 | tf_op jit(solution)/shard_map/ppermute | solution.py:716
  728.4 45.1 %collective-permute-start.2 = (bf16[960,1024]{1,0:T(8,128)(2,1)}, bf16[960,1024]{1,0:T(8,128)(2,1)}, u32[]{:S(2)}, u32[]{:S(2)}) collective-permute-start(bf16[960,1024]{1,0:T(8,128)(2,1)} %collective-permute-done.1.refs_8_), channel_id=1, source_target_pairs={{0,2},{1,3},{2,0},{3,1},{4,6},{5,7},{6,4},{7,5},{8,10},{9,11},{10,... | collective-permute-start | bytes 5898248 | tf_op jit(solution)/shard_map/ppermute | solution.py:716
  731.6 45.2 %collective-permute-start.3 = (bf16[960,1024]{1,0:T(8,128)(2,1)}, bf16[960,1024]{1,0:T(8,128)(2,1)}, u32[]{:S(2)}, u32[]{:S(2)}) collective-permute-start(bf16[960,1024]{1,0:T(8,128)(2,1)} %collective-permute-done.refs_5_), channel_id=1, source_target_pairs={{0,4},{1,5},{2,6},{3,7},{4,0},{5,1},{6,2},{7,3},{8,12},{9,13},{10,... | collective-permute-start | bytes 5898248 | tf_op jit(solution)/shard_map/ppermute | solution.py:716
  776.8 4.3 collective-permute-start.12
  776.8 7.1 collective-permute-start.13

commit v6 on v5

--- a/solution.py
+++ b/solution.py
@@ -476,20 +476,22 @@
     forward(slab_view(ring), ring, tail)
     for index in range(ring - 2 * LAG, ring):
         forward_diagonal(slab_view(index), index, chunk)
+        if index == ring - 2:
+            for older in range(ring - RETIRE, ring - LAG):
+                retire(older)
+            for older in range(ring, last):
+                finish_exchange(older, chunk)
+            finish_exchange(last, plan.tail_window)
+            whole_finish()
+            for n, own in enumerate((own_0, own_1)):
+                wait_for(own.at[:, pl.ds(0, plan.cut)], share_recv.at[n])
+                for parts in (8, 5):
+                    sent = pl.ds(0, parts * (plan.down_rows + plan.out_rows))
+                    wait_for(own.at[sent, pl.ds(0, plan.cut)], share_send.at[n])
     forward_diagonal(slab_view(ring), ring, tail)
-
-    for index in range(ring - RETIRE, ring):
+    for index in range(ring - LAG, ring):
         retire(index)
     finish(slab_view(ring), ring, tail)
-    for index in range(ring, last):
-        finish_exchange(index, chunk)
-    finish_exchange(last, plan.tail_window)
-    whole_finish()
-    for n, own in enumerate((own_0, own_1)):
-        wait_for(own.at[:, pl.ds(0, plan.cut)], share_recv.at[n])
-        for parts in (8, 5):
-            sent = pl.ds(0, parts * (plan.down_rows + plan.out_rows))
-            wait_for(own.at[sent, pl.ds(0, plan.cut)], share_send.at[n])
 
 
 def gather(plan, *args):
@@ -686,16 +688,15 @@
 
 
 def place_shares(plan, shares, held):
-    owners = list(shares)
-    arrays = [array for owner in owners for array in shares[owner]]
+    which = [(owner, part) for owner, arrays in shares.items() for part in arrays]
+    arrays = [shares[owner][part] for owner, part in which]
 
     def spots(refs, dp):
         core, x, y = dp % 2, (dp // 2) % 2, dp // 4
         found = []
-        for n, ref in enumerate(refs):
-            flip_x, flip_y, flip_core = owners[n // plan.share]
+        for ref, ((flip_x, flip_y, flip_core), part) in zip(refs, which, strict=True):
             owner = (y + flip_y * (1 - 2 * y)) * 4 + (x + flip_x * (1 - 2 * x)) * 2 + core + flip_core * (1 - 2 * core)
-            found.append((ref, owner * plan.share + n % plan.share, owner, n % plan.share))
+            found.append((ref, owner * plan.share + part, owner, part))
         return found
 
     return place_rows(plan, arrays, spots, plan.cut, plan.whole, held)
@@ -736,14 +737,19 @@
         head_block = place_head(plan, slabs, 0, early, head_block)
         own_0, own_1, head_block = hold((own_0, own_1, head_block))
         near = {
-            (0, 0, 0): [own_0, own_1], (0, 0, 1): pair_own, (1, 0, 0): [x_0, x_1], (1, 0, 1): [pair_x_0, pair_x_1],
-            (0, 1, 0): [y_0, y_1], (0, 1, 1): [pair_y_0, pair_y_1],
+            (0, 0, 0): {0: own_0, 1: own_1}, (0, 0, 1): dict(enumerate(pair_own)),
+            (1, 0, 0): {0: x_0, 1: x_1}, (1, 0, 1): {0: pair_x_0, 1: pair_x_1},
+            (0, 1, 0): {0: y_0, 1: y_1}, (0, 1, 1): {0: pair_y_0, 1: pair_y_1},
         }
         placed = place_shares(plan, near, {0: placed[0], 1: placed[1], 2: head_block})
-        diagonal_0, diagonal_1, *placed = hold((diagonal_0, diagonal_1, placed[0], placed[1], placed[2]))
-        pair_diagonal = [pair(diagonal_0), pair(diagonal_1)]
-        placed = place_shares(plan, {(1, 1, 0): [diagonal_0, diagonal_1]}, dict(enumerate(placed)))
-        placed = place_shares(plan, {(1, 1, 1): pair_diagonal}, placed)
+        diagonal_0, head_block = hold((diagonal_0, placed[2]))
+        pair_diagonal_0 = pair(diagonal_0)
+        diagonal_1, down_block = hold((diagonal_1, placed[0]))
+        pair_diagonal_1 = pair(diagonal_1)
+        placed = {0: down_block, 1: placed[1], 2: head_block}
+        placed = place_shares(plan, {(1, 1, 0): {0: diagonal_0, 1: diagonal_1}}, placed)
+        placed = place_shares(plan, {(1, 1, 1): {0: pair_diagonal_0}}, placed)
+        placed = place_shares(plan, {(1, 1, 1): {1: pair_diagonal_1}}, placed)
         down_block, o_block, head_block = placed[0], placed[1], placed[2]
         return (
             qkv_block,

time: 788 us -> 786 us (level)
    pallas_call x4 -> x5, Pallas kernels: 33.4 us -> 35.5 us  [place_rows(): pl.pallas_call(body, out_shape=[outs[n] for n in made], in_specs=[hbm] *...]
  transfers between devices with their start and end apart: 14 -> 14, of which waited for: 7 -> 5; matrix products, arithmetic and copies ran while one was open for 0% -> 0% of each run, Pallas kernels for 15% -> 16%
where the time goes in v6:
time: 786 us
  Pallas kernels  763 us (97%)
  waiting for transfers between devices  16.2 us (2%)
    pallas_call x1, Pallas kernels, gather(): pl.pallas_call(functools.partial(gather_kernel, plan), out_shape=[jax.Sha...  637 us
    pallas_call x3, Pallas kernels, place_slabs(): pl.pallas_call(body, in_specs=[hbm] * (1 + len(held)), out_specs=[hbm] *...  89.8 us
    pallas_call x5, Pallas kernels, place_rows(): pl.pallas_call(body, out_shape=[outs[n] for n in made], in_specs=[hbm] *...  35.5 us
    ppermute x14, waiting for transfers between devices, swap(): return lax.ppermute(array, 'dp', [(i, i ^ bit) for i in range(plan.dp)])  16.2 us
  transfers between devices with their start and end apart: 14, of which 5 were waited for; matrix products, arithmetic and copies ran while one was open for 0% of the time, Pallas kernels for 16%

profile of v6, /device:TPU:0, one launch (start us, length us, event | category | flops | bytes accessed | tf_op | source)
XLA Modules:
  0.0 786.3 jit_solution(10139184915283709758)
XLA Ops:
  0.6 637.2 %gather.1 = (bf16[8,31,2176,128]{3,2,1,0:T(8,128)(2,1)}, bf16[960,1024]{1,0:T(8,128)(2,1)}, bf16[960,1024]{1,0:T(8,128)(2,1)}, bf16[16,960,384]{2,1,0:T(8,128)(2...) custom-call(bf16[16,32,1024]{2,1,0:T(8,128)(2,1)} %q.1, ...), custom_call_target="tpu_custom_call" | custom-call | tf_op jit(solution)/shard_map/gather/pallas_call | solution.py:505
  637.8 2.3 collective-permute-start
  640.1 0.0 collective-permute-start.1
  640.2 1.9 collective-permute-start.3
  642.1 0.1 collective-permute-start.4
  642.2 45.5 %shard_map.119 = (bf16[16,768,1024]{2,1,0:T(8,128)(2,1)}, bf16[16,1408,1024]{2,1,0:T(8,128)(2,1)}) custom-call(bf16[8,31,2176,128]{3,2,1,0:T(8,128)(2,1)} %get-tuple-element.56.slab), custom_call_target="tpu_custom_call" | custom-call | flops 10000000 | bytes 142606336 | tf_op jit(solution)/shard_map/pallas_call | solution.py:578
  687.7 0.6 collective-permute-start.6
  688.3 34.0 %shard_map.120.refs_0_ = bf16[37984,1024]{1,0:T(8,128)(2,1)} custom-call(bf16[8,31,2176,128]{3,2,1,0:T(8,128)(2,1)} %get-tuple-element.56.slab), custom_call_target="tpu_custom_call" | custom-call | flops 10000000 | bytes 106954752 | tf_op jit(solution)/shard_map/pallas_call | solution.py:578
  722.3 3.6 collective-permute-done.3.refs_4_
  725.9 1.5 collective-permute-done.4.refs_9_
  727.3 0.5 collective-permute-start.7
  727.8 0.0 collective-permute-start.8
  727.9 0.5 collective-permute-start.9
  728.4 0.4 collective-permute-start.12
  728.7 2.9 collective-permute-done.10.refs_11_
  731.7 0.3 collective-permute-start.2
  732.0 9.4 %shard_map.121 = (bf16[16,704,1024]{2,1,0:T(8,128)(2,1)}, bf16[16,1024,256]{2,1,0:T(8,128)(2,1)}) custom-call(bf16[16,960,384]{2,1,0:T(8,128)(2,1)} %get-tuple-element.53.refs_0_), custom_call_target="tpu_custom_call" | custom-call | flops 10000000 | bytes 23592960 | tf_op jit(solution)/shard_map/pallas_call | solution.py:666
  741.4 10.4 %shard_map.122.refs_14_ = bf16[37984,1024]{1,0:T(8,128)(2,1)} custom-call(bf16[8,31,2176,128]{3,2,1,0:T(8,128)(2,1)} %get-tuple-element.56.slab, bf16[37984,1024]{1,0:T(8,128)(2,1)} %shard_map.120.refs_0_), custom_call_target="tpu_custom_call", output_to_operand_aliasing={{}: (1, {})} | custom-call | flops 10000000 | bytes 26738688 | tf_op jit(solution)/shard_map/pallas_call | solution.py:578
  751.8 16.8 %shard_map.123 = (bf16[16,704,1024]{2,1,0:T(8,128)(2,1)}, bf16[16,1024,256]{2,1,0:T(8,128)(2,1)}, bf16[37984,1024]{1,0:T(8,128)(2,1)}) custom-call(bf16[960,1024]{1,0:T(8,128)(2,1)} %get-tuple-element.58.refs_0_, bf16[960,1024]{1,0:T(8,128)(2,1)} %get-tuple-element.59.refs_1_, ...), custom_call_target="tpu_custom_call", output_to_operand_aliasing={{0}: (12, {}), {1}: (13, {}), {2}: (14, {})} | custom-call | flops 10000000 | bytes 47185920 | tf_op jit(solution)/shard_map/pallas_call | solution.py:666
  768.6 4.9 collective-permute-done.12.refs_0_
  773.5 3.3 collective-permute-done.2.refs_1_
  776.8 3.6 shard_map.124
  780.5 2.9 shard_map.125
  783.4 2.9 shard_map.126
  (13 shorter events, 0.0 us)
Async XLA Ops:
  637.8 49.9 %collective-permute-start = (bf16[960,1024]{1,0:T(8,128)(2,1)}, bf16[960,1024]{1,0:T(8,128)(2,1)}, u32[]{:S(2)}, u32[]{:S(2)}) collective-permute-start(bf16[960,1024]{1,0:T(8,128)(2,1)} %get-tuple-element.59.refs_1_), channel_id=1, source_target_pairs={{0,2},{1,3},{2,0},{3,1},{4,6},{5,7},{6,4},{7,5},{8,10},{9,11},{10,... | collective-permute-start | bytes 5898248 | tf_op jit(solution)/shard_map/ppermute | solution.py:717
  640.1 48.2 %collective-permute-start.1 = (bf16[960,1024]{1,0:T(8,128)(2,1)}, bf16[960,1024]{1,0:T(8,128)(2,1)}, u32[]{:S(2)}, u32[]{:S(2)}) collective-permute-start(bf16[960,1024]{1,0:T(8,128)(2,1)} %get-tuple-element.58.refs_0_), channel_id=1, source_target_pairs={{0,4},{1,5},{2,6},{3,7},{4,0},{5,1},{6,2},{7,3},{8,12},{9,13},{10,... | collective-permute-start | bytes 5898248 | tf_op jit(solution)/shard_map/ppermute | solution.py:717
  640.2 85.7 %collective-permute-start.3 = (bf16[960,1024]{1,0:T(8,128)(2,1)}, bf16[960,1024]{1,0:T(8,128)(2,1)}, u32[]{:S(2)}, u32[]{:S(2)}) collective-permute-start(bf16[960,1024]{1,0:T(8,128)(2,1)} %get-tuple-element.58.refs_0_), channel_id=1, source_target_pairs={{0,2},{1,3},{2,0},{3,1},{4,6},{5,7},{6,4},{7,5},{8,10},{9,11},{10,... | collective-permute-start | bytes 5898248 | tf_op jit(solution)/shard_map/ppermute | solution.py:717
  642.1 85.2 %collective-permute-start.4 = (bf16[960,1024]{1,0:T(8,128)(2,1)}, bf16[960,1024]{1,0:T(8,128)(2,1)}, u32[]{:S(2)}, u32[]{:S(2)}) collective-permute-start(bf16[960,1024]{1,0:T(8,128)(2,1)} %get-tuple-element.59.refs_1_), channel_id=1, source_target_pairs={{0,4},{1,5},{2,6},{3,7},{4,0},{5,1},{6,2},{7,3},{8,12},{9,13},{10,... | collective-permute-start | bytes 5898248 | tf_op jit(solution)/shard_map/ppermute | solution.py:717
  642.2 85.6 %collective-permute-start.5 = (bf16[960,1024]{1,0:T(8,128)(2,1)}, bf16[960,1024]{1,0:T(8,128)(2,1)}, u32[]{:S(2)}, u32[]{:S(2)}) collective-permute-start(bf16[960,1024]{1,0:T(8,128)(2,1)} %get-tuple-element.58.refs_0_), channel_id=1, source_target_pairs={{0,1},{1,0},{2,3},{3,2},{4,5},{5,4},{6,7},{7,6},{8,9},{9,8},{10,11... | collective-permute-start | bytes 5898248 | tf_op jit(solution)/shard_map/ppermute | solution.py:717
  687.7 40.6 %collective-permute-start.6 = (bf16[960,1024]{1,0:T(8,128)(2,1)}, bf16[960,1024]{1,0:T(8,128)(2,1)}, u32[]{:S(2)}, u32[]{:S(2)}) collective-permute-start(bf16[960,1024]{1,0:T(8,128)(2,1)} %get-tuple-element.59.refs_1_), channel_id=1, source_target_pairs={{0,1},{1,0},{2,3},{3,2},{4,5},{5,4},{6,7},{7,6},{8,9},{9,8},{10,11... | collective-permute-start | bytes 5898248 | tf_op jit(solution)/shard_map/ppermute | solution.py:717
  727.3 4.3 collective-permute-start.10
  727.3 24.4 %collective-permute-start.7 = (bf16[960,1024]{1,0:T(8,128)(2,1)}, bf16[960,1024]{1,0:T(8,128)(2,1)}, u32[]{:S(2)}, u32[]{:S(2)}) collective-permute-start(bf16[960,1024]{1,0:T(8,128)(2,1)} %collective-permute-done.3.refs_4_), channel_id=1, source_target_pairs={{0,1},{1,0},{2,3},{3,2},{4,5},{5,4},{6,7},{7,6},{8,9},{9,8},{10,11... | collective-permute-start | bytes 5898248 | tf_op jit(solution)/shard_map/ppermute | solution.py:717
  727.8 23.9 %collective-permute-start.8 = (bf16[960,1024]{1,0:T(8,128)(2,1)}, bf16[960,1024]{1,0:T(8,128)(2,1)}, u32[]{:S(2)}, u32[]{:S(2)}) collective-permute-start(bf16[960,1024]{1,0:T(8,128)(2,1)} %collective-permute-done.refs_5_), channel_id=1, source_target_pairs={{0,1},{1,0},{2,3},{3,2},{4,5},{5,4},{6,7},{7,6},{8,9},{9,8},{10,11... | collective-permute-start | bytes 5898248 | tf_op jit(solution)/shard_map/ppermute | solution.py:717
  727.9 23.9 %collective-permute-start.9 = (bf16[960,1024]{1,0:T(8,128)(2,1)}, bf16[960,1024]{1,0:T(8,128)(2,1)}, u32[]{:S(2)}, u32[]{:S(2)}) collective-permute-start(bf16[960,1024]{1,0:T(8,128)(2,1)} %collective-permute-done.1.refs_8_), channel_id=1, source_target_pairs={{0,1},{1,0},{2,3},{3,2},{4,5},{5,4},{6,7},{7,6},{8,9},{9,8},{10,11... | collective-permute-start | bytes 5898248 | tf_op jit(solution)/shard_map/ppermute | solution.py:717
  728.4 45.1 %collective-permute-start.12 = (bf16[960,1024]{1,0:T(8,128)(2,1)}, bf16[960,1024]{1,0:T(8,128)(2,1)}, u32[]{:S(2)}, u32[]{:S(2)}) collective-permute-start(bf16[960,1024]{1,0:T(8,128)(2,1)} %collective-permute-done.1.refs_8_), channel_id=1, source_target_pairs={{0,2},{1,3},{2,0},{3,1},{4,6},{5,7},{6,4},{7,5},{8,10},{9,11},{10,... | collective-permute-start | bytes 5898248 | tf_op jit(solution)/shard_map/ppermute | solution.py:717
  731.7 45.2 %collective-permute-start.2 = (bf16[960,1024]{1,0:T(8,128)(2,1)}, bf16[960,1024]{1,0:T(8,128)(2,1)}, u32[]{:S(2)}, u32[]{:S(2)}) collective-permute-start(bf16[960,1024]{1,0:T(8,128)(2,1)} %collective-permute-done.refs_5_), channel_id=1, source_target_pairs={{0,4},{1,5},{2,6},{3,7},{4,0},{5,1},{6,2},{7,3},{8,12},{9,13},{10,... | collective-permute-start | bytes 5898248 | tf_op jit(solution)/shard_map/ppermute | solution.py:717
  773.5 7.0 collective-permute-start.13
  776.8 6.5 collective-permute-start.11

commit v7 on v6

--- a/solution.py
+++ b/solution.py
@@ -15,7 +15,8 @@
 BUFFERS = 6
 LAG = 2
 SHARE_AT = 20
-RETIRE = 8
+SLOTS = 8
+COUNTED = 4
 WHOLE = 3
 WHOLE_AT = 2
 RANKS_AT = 10
@@ -50,6 +51,7 @@
         self.extra_first = self.vocab - self.share * WHOLE * self.piece
         self.ring = self.layers + self.extra_first // self.chunk
         self.tail = self.extra_first % self.chunk
+        self.counts = -(-self.ring // COUNTED) + 1
 
     def wide_base(self, rank):
         return (self.wide * rank) // LANES
@@ -83,6 +85,9 @@
         pltpu.make_async_copy(ref, ref, sem).wait()
 
 
+    def z_slot(index):
+        return index - layers + layers // GROUP
+
     def rank_at(step):
         return (z + step + core * (plan.tp - 2 * step)) % plan.tp
 
@@ -105,23 +110,24 @@
                 pltpu.make_async_copy(source, target, pack_sem.at[group]).start()
         for source, column, width in layer_pieces(group * GROUP, z):
             target = zbuf.at[pl.ds(group * GROUP, GROUP), my_rows, pl.ds(column, width)]
-            pltpu.make_async_copy(source, target, z_recv.at[group * GROUP]).start()
+            pltpu.make_async_copy(source, target, z_recv.at[group]).start()
 
     def exchange_layers(group):
         wait_for(packed.at[group], pack_sem.at[group])
         for step in range(1, plan.tp):
             index = group * GROUP
             target = zbuf.at[pl.ds(index, GROUP), my_rows, :]
-            remote(packed.at[group, step - 1], target, z_send.at[index], z_recv.at[index], tp=rank_at(step))
+            remote(packed.at[group, step - 1], target, z_send.at[0], z_recv.at[group], tp=rank_at(step))
 
     def exchange_head(index, width):
         def piece(rank):
             return h.at[:, lanes(plan.head_base(rank) + (index - layers) * (chunk // LANES), width)]
 
         target = zbuf.at[index, my_rows, pl.ds(0, width)]
+        sent = z_send.at[1 if width == chunk else 2]
         for step in range(1, plan.tp):
-            remote(piece(rank_at(step)), target, z_send.at[index], z_recv.at[index], tp=rank_at(step))
-        pltpu.make_async_copy(piece(z), target, z_recv.at[index]).start()
+            remote(piece(rank_at(step)), target, sent, z_recv.at[z_slot(index)], tp=rank_at(step))
+        pltpu.make_async_copy(piece(z), target, z_recv.at[z_slot(index)]).start()
 
     def start_exchange(index):
         @pl.when((index >= layers) & (index < last))
@@ -133,7 +139,7 @@
             exchange_head(last, plan.tail_window)
 
     def wait_exchange(index, width):
-        wait_for(zbuf.at[index, :, pl.ds(0, width)], z_recv.at[index])
+        wait_for(zbuf.at[index, :, pl.ds(0, width)], z_recv.at[z_slot(index)])
 
 
     def turn(slot, tile, index, source_tile):
@@ -147,7 +153,7 @@
     def make_layer(index, slot):
         @pl.when(index % GROUP == 0)
         def _():
-            wait_for(zbuf.at[pl.ds(index, GROUP), :, pl.ds(0, plan.layer_window)], z_recv.at[index])
+            wait_for(zbuf.at[pl.ds(index, GROUP), :, pl.ds(0, plan.layer_window)], z_recv.at[index // GROUP])
 
         for tile in range(plan.layer_window // LANES):
             turn(slot, tile, index, tile)
@@ -209,36 +215,41 @@
         return lambda owner, first, count: slabs.at[owner, index, pl.ds(first, count), :]
 
     def push(part, index, recv, to):
-        remote(part, part, send.at[index], recv.at[index], dp=to)
+        remote(part, part, send.at[counted(index)], recv.at[index % SLOTS], dp=to)
+
+    def push_pair(part, index):
+        remote(part, part, send.at[counted(index)], pair_recv.at[counted(index)], dp=pair)
+
+    def counted(index):
+        return index // COUNTED if index is not ring else plan.counts - 1
 
     def send_own(view, index, slot, count):
         own = view(dp, 0, count)
         wait_for(own, local.at[slot])
         push(own, index, x_recv, x_peer)
         push(own, index, y_recv, y_peer)
-        push(own, index, pair_recv, pair)
+        push_pair(own, index)
 
     def forward(view, index, count):
         half = count // 2
-        wait_for(view(x_peer, 0, count), x_recv.at[index])
+        slot = index % SLOTS
+        wait_for(view(x_peer, 0, count), x_recv.at[slot])
         push(view(x_peer, half, half), index, b_recv, y_peer)
-        push(view(x_peer, 0, count), index, pair_recv, pair)
-        wait_for(view(y_peer, 0, count), y_recv.at[index])
+        push_pair(view(x_peer, 0, count), index)
+        wait_for(view(y_peer, 0, count), y_recv.at[slot])
         push(view(y_peer, 0, half), index, a_recv, x_peer)
-        push(view(y_peer, 0, count), index, pair_recv, pair)
+        push_pair(view(y_peer, 0, count), index)
 
     def forward_diagonal(view, index, count):
         half = count // 2
-        wait_for(view(diagonal, 0, half), a_recv.at[index])
-        wait_for(view(diagonal, half, half), b_recv.at[index])
-        push(view(diagonal, 0, count), index, pair_recv, pair)
-
-    def finish(view, index, count):
-        wait_for(view(pl.ds(0, 7), 0, count), send.at[index])
-        wait_for(view(pl.ds(0, 4), 0, count), pair_recv.at[index])
-
-    def finish_exchange(index, window):
-        wait_for(zbuf.at[index, pl.ds(0, (plan.tp - 1) * rows), pl.ds(0, window)], z_send.at[index])
+        slot = index % SLOTS
+        wait_for(view(diagonal, 0, half), a_recv.at[slot])
+        wait_for(view(diagonal, half, half), b_recv.at[slot])
+        push_pair(view(diagonal, 0, count), index)
+
+    def finish(index, some, count):
+        wait_for(slabs.at[pl.ds(0, 7), some, pl.ds(0, count), :], send.at[index])
+        wait_for(slabs.at[pl.ds(0, 4), some, pl.ds(0, count), :], pair_recv.at[index])
 
 
     def pieces(source_dp, to, place):
@@ -404,18 +415,6 @@
     for index in range(layers, AHEAD):
         start_exchange(index)
 
-    def retire(index):
-        finish(slab_view(index), index, chunk)
-
-        @pl.when((index < layers) & (index % GROUP == 0))
-        def _():
-            sent = pl.ds(0, (plan.tp - 1) * rows)
-            wait_for(zbuf.at[pl.ds(index, GROUP), sent, pl.ds(0, plan.layer_window)], z_send.at[index])
-
-        @pl.when(index >= layers)
-        def _():
-            finish_exchange(index, chunk)
-
     def step(index, _):
         slot = index % 2
 
@@ -457,10 +456,6 @@
         @pl.when(index >= 2 * LAG)
         def _():
             forward_diagonal(slab_view(index - 2 * LAG), index - 2 * LAG, chunk)
-
-        @pl.when(index >= RETIRE)
-        def _():
-            retire(index - RETIRE)
 
         return 0
 
@@ -477,26 +472,28 @@
     for index in range(ring - 2 * LAG, ring):
         forward_diagonal(slab_view(index), index, chunk)
         if index == ring - 2:
-            for older in range(ring - RETIRE, ring - LAG):
-                retire(older)
-            for older in range(ring, last):
-                finish_exchange(older, chunk)
-            finish_exchange(last, plan.tail_window)
+            sent = pl.ds(0, (plan.tp - 1) * rows)
+            wait_for(packed, z_send.at[0])
+            wait_for(zbuf.at[pl.ds(layers, last - layers), sent, pl.ds(0, chunk)], z_send.at[1])
+            wait_for(zbuf.at[last, sent, pl.ds(0, plan.tail_window)], z_send.at[2])
             whole_finish()
             for n, own in enumerate((own_0, own_1)):
                 wait_for(own.at[:, pl.ds(0, plan.cut)], share_recv.at[n])
                 for parts in (8, 5):
-                    sent = pl.ds(0, parts * (plan.down_rows + plan.out_rows))
-                    wait_for(own.at[sent, pl.ds(0, plan.cut)], share_send.at[n])
+                    gone = pl.ds(0, parts * (plan.down_rows + plan.out_rows))
+                    wait_for(own.at[gone, pl.ds(0, plan.cut)], share_send.at[n])
+            for index in range((ring - LAG) // COUNTED):
+                finish(index, pl.ds(index * COUNTED, COUNTED), chunk)
     forward_diagonal(slab_view(ring), ring, tail)
-    for index in range(ring - LAG, ring):
-        retire(index)
-    finish(slab_view(ring), ring, tail)
+    for index in range((ring - LAG) // COUNTED, plan.counts - 1):
+        first = index * COUNTED
+        finish(index, pl.ds(first, min(COUNTED, ring - first)), chunk)
+    finish(plan.counts - 1, pl.ds(ring, 1), tail)
 
 
 def gather(plan, *args):
     dma = pltpu.SemaphoreType.DMA
-    per_chunk = dma((plan.chunks,))
+    groups = plan.layers // GROUP
     share_rows = plan.down_rows + plan.out_rows
     hbm = pl.BlockSpec(memory_space=pltpu.HBM)
     shapes = [(plan.dp, plan.ring + 1, plan.chunk, LANES), (plan.piece, plan.columns), (plan.piece, plan.columns)]
@@ -510,8 +507,8 @@
         scratch_shapes=[
             pltpu.VMEM((plan.chunks, plan.tp * plan.rows, plan.layer_window), jnp.bfloat16),
             pltpu.VMEM((2, plan.chunk + 2 * LANES, LANES), jnp.bfloat16),
-            per_chunk, per_chunk, dma((2,)),
-            per_chunk, per_chunk, per_chunk, per_chunk, per_chunk, per_chunk,
+            dma((groups + plan.head_chunks,)), dma((3,)), dma((2,)),
+            dma((SLOTS,)), dma((SLOTS,)), dma((SLOTS,)), dma((SLOTS,)), dma((plan.counts,)), dma((plan.counts,)),
             dma((2, plan.dp)), dma((2,)), dma((2,)),
             dma((8,)), dma((2,)), dma((2,)), dma((2,)), dma((2,)), dma((2,)),
             pltpu.VMEM((plan.layers, plan.down_rows, plan.whole), jnp.bfloat16),

time: 786 us -> 785 us (level)
  no operation moved by 1% of the time
where the time goes in v7:
time: 785 us
  Pallas kernels  761 us (97%)
  waiting for transfers between devices  16.2 us (2%)
    pallas_call x1, Pallas kernels, gather(): pl.pallas_call(functools.partial(gather_kernel, plan), out_shape=[jax.Sha...  635 us
    pallas_call x3, Pallas kernels, place_slabs(): pl.pallas_call(body, in_specs=[hbm] * (1 + len(held)), out_specs=[hbm] *...  89.8 us
    pallas_call x5, Pallas kernels, place_rows(): pl.pallas_call(body, out_shape=[outs[n] for n in made], in_specs=[hbm] *...  35.5 us
    ppermute x14, waiting for transfers between devices, swap(): return lax.ppermute(array, 'dp', [(i, i ^ bit) for i in range(plan.dp)])  16.2 us
  transfers between devices with their start and end apart: 14, of which 5 were waited for; matrix products, arithmetic and copies ran while one was open for 0% of the time, Pallas kernels for 16%

profile of v7, /device:TPU:0, one launch (start us, length us, event | category | flops | bytes accessed | tf_op | source)
XLA Modules:
  0.0 784.5 jit_solution(9175382835329387079)
XLA Ops:
  0.6 635.4 %gather.1 = (bf16[8,31,2176,128]{3,2,1,0:T(8,128)(2,1)}, bf16[960,1024]{1,0:T(8,128)(2,1)}, bf16[960,1024]{1,0:T(8,128)(2,1)}, bf16[16,960,384]{2,1,0:T(8,128)(2...) custom-call(bf16[16,32,1024]{2,1,0:T(8,128)(2,1)} %q.1, ...), custom_call_target="tpu_custom_call" | custom-call | tf_op jit(solution)/shard_map/gather/pallas_call | solution.py:502
  636.0 2.3 collective-permute-start
  638.4 0.0 collective-permute-start.1
  638.4 1.9 collective-permute-start.3
  640.4 0.1 collective-permute-start.4
  640.5 45.5 %shard_map.119 = (bf16[16,768,1024]{2,1,0:T(8,128)(2,1)}, bf16[16,1408,1024]{2,1,0:T(8,128)(2,1)}) custom-call(bf16[8,31,2176,128]{3,2,1,0:T(8,128)(2,1)} %get-tuple-element.56.slab), custom_call_target="tpu_custom_call" | custom-call | flops 10000000 | bytes 142606336 | tf_op jit(solution)/shard_map/pallas_call | solution.py:575
  686.0 0.6 collective-permute-start.6
  686.5 34.0 %shard_map.120.refs_0_ = bf16[37984,1024]{1,0:T(8,128)(2,1)} custom-call(bf16[8,31,2176,128]{3,2,1,0:T(8,128)(2,1)} %get-tuple-element.56.slab), custom_call_target="tpu_custom_call" | custom-call | flops 10000000 | bytes 106954752 | tf_op jit(solution)/shard_map/pallas_call | solution.py:575
  720.5 3.6 collective-permute-done.3.refs_4_
  724.1 1.5 collective-permute-done.4.refs_9_
  725.6 0.5 collective-permute-start.7
  726.1 0.0 collective-permute-start.8
  726.1 0.5 collective-permute-start.9
  726.6 0.4 collective-permute-start.12
  727.0 2.9 collective-permute-done.10.refs_11_
  729.9 0.3 collective-permute-start.2
  730.2 9.4 %shard_map.121 = (bf16[16,704,1024]{2,1,0:T(8,128)(2,1)}, bf16[16,1024,256]{2,1,0:T(8,128)(2,1)}) custom-call(bf16[16,960,384]{2,1,0:T(8,128)(2,1)} %get-tuple-element.53.refs_0_), custom_call_target="tpu_custom_call" | custom-call | flops 10000000 | bytes 23592960 | tf_op jit(solution)/shard_map/pallas_call | solution.py:663
  739.6 10.4 %shard_map.122.refs_14_ = bf16[37984,1024]{1,0:T(8,128)(2,1)} custom-call(bf16[8,31,2176,128]{3,2,1,0:T(8,128)(2,1)} %get-tuple-element.56.slab, bf16[37984,1024]{1,0:T(8,128)(2,1)} %shard_map.120.refs_0_), custom_call_target="tpu_custom_call", output_to_operand_aliasing={{}: (1, {})} | custom-call | flops 10000000 | bytes 26738688 | tf_op jit(solution)/shard_map/pallas_call | solution.py:575
  750.0 16.8 %shard_map.123 = (bf16[16,704,1024]{2,1,0:T(8,128)(2,1)}, bf16[16,1024,256]{2,1,0:T(8,128)(2,1)}, bf16[37984,1024]{1,0:T(8,128)(2,1)}) custom-call(bf16[960,1024]{1,0:T(8,128)(2,1)} %get-tuple-element.58.refs_0_, bf16[960,1024]{1,0:T(8,128)(2,1)} %get-tuple-element.59.refs_1_, ...), custom_call_target="tpu_custom_call", output_to_operand_aliasing={{0}: (12, {}), {1}: (13, {}), {2}: (14, {})} | custom-call | flops 10000000 | bytes 47185920 | tf_op jit(solution)/shard_map/pallas_call | solution.py:663
  766.8 4.9 collective-permute-done.12.refs_0_
  771.7 3.3 collective-permute-done.2.refs_1_
  775.1 3.6 shard_map.124
  778.7 2.9 shard_map.125
  781.6 2.9 shard_map.126
  (13 shorter events, 0.0 us)
Async XLA Ops:
  636.0 49.9 %collective-permute-start = (bf16[960,1024]{1,0:T(8,128)(2,1)}, bf16[960,1024]{1,0:T(8,128)(2,1)}, u32[]{:S(2)}, u32[]{:S(2)}) collective-permute-start(bf16[960,1024]{1,0:T(8,128)(2,1)} %get-tuple-element.59.refs_1_), channel_id=1, source_target_pairs={{0,2},{1,3},{2,0},{3,1},{4,6},{5,7},{6,4},{7,5},{8,10},{9,11},{10,... | collective-permute-start | bytes 5898248 | tf_op jit(solution)/shard_map/ppermute | solution.py:714
  638.4 48.2 %collective-permute-start.1 = (bf16[960,1024]{1,0:T(8,128)(2,1)}, bf16[960,1024]{1,0:T(8,128)(2,1)}, u32[]{:S(2)}, u32[]{:S(2)}) collective-permute-start(bf16[960,1024]{1,0:T(8,128)(2,1)} %get-tuple-element.58.refs_0_), channel_id=1, source_target_pairs={{0,4},{1,5},{2,6},{3,7},{4,0},{5,1},{6,2},{7,3},{8,12},{9,13},{10,... | collective-permute-start | bytes 5898248 | tf_op jit(solution)/shard_map/ppermute | solution.py:714
  638.4 85.7 %collective-permute-start.3 = (bf16[960,1024]{1,0:T(8,128)(2,1)}, bf16[960,1024]{1,0:T(8,128)(2,1)}, u32[]{:S(2)}, u32[]{:S(2)}) collective-permute-start(bf16[960,1024]{1,0:T(8,128)(2,1)} %get-tuple-element.58.refs_0_), channel_id=1, source_target_pairs={{0,2},{1,3},{2,0},{3,1},{4,6},{5,7},{6,4},{7,5},{8,10},{9,11},{10,... | collective-permute-start | bytes 5898248 | tf_op jit(solution)/shard_map/ppermute | solution.py:714
  640.4 85.2 %collective-permute-start.4 = (bf16[960,1024]{1,0:T(8,128)(2,1)}, bf16[960,1024]{1,0:T(8,128)(2,1)}, u32[]{:S(2)}, u32[]{:S(2)}) collective-permute-start(bf16[960,1024]{1,0:T(8,128)(2,1)} %get-tuple-element.59.refs_1_), channel_id=1, source_target_pairs={{0,4},{1,5},{2,6},{3,7},{4,0},{5,1},{6,2},{7,3},{8,12},{9,13},{10,... | collective-permute-start | bytes 5898248 | tf_op jit(solution)/shard_map/ppermute | solution.py:714
  640.5 85.6 %collective-permute-start.5 = (bf16[960,1024]{1,0:T(8,128)(2,1)}, bf16[960,1024]{1,0:T(8,128)(2,1)}, u32[]{:S(2)}, u32[]{:S(2)}) collective-permute-start(bf16[960,1024]{1,0:T(8,128)(2,1)} %get-tuple-element.58.refs_0_), channel_id=1, source_target_pairs={{0,1},{1,0},{2,3},{3,2},{4,5},{5,4},{6,7},{7,6},{8,9},{9,8},{10,11... | collective-permute-start | bytes 5898248 | tf_op jit(solution)/shard_map/ppermute | solution.py:714
  686.0 40.6 %collective-permute-start.6 = (bf16[960,1024]{1,0:T(8,128)(2,1)}, bf16[960,1024]{1,0:T(8,128)(2,1)}, u32[]{:S(2)}, u32[]{:S(2)}) collective-permute-start(bf16[960,1024]{1,0:T(8,128)(2,1)} %get-tuple-element.59.refs_1_), channel_id=1, source_target_pairs={{0,1},{1,0},{2,3},{3,2},{4,5},{5,4},{6,7},{7,6},{8,9},{9,8},{10,11... | collective-permute-start | bytes 5898248 | tf_op jit(solution)/shard_map/ppermute | solution.py:714
  725.6 4.3 collective-permute-start.10
  725.6 24.4 %collective-permute-start.7 = (bf16[960,1024]{1,0:T(8,128)(2,1)}, bf16[960,1024]{1,0:T(8,128)(2,1)}, u32[]{:S(2)}, u32[]{:S(2)}) collective-permute-start(bf16[960,1024]{1,0:T(8,128)(2,1)} %collective-permute-done.3.refs_4_), channel_id=1, source_target_pairs={{0,1},{1,0},{2,3},{3,2},{4,5},{5,4},{6,7},{7,6},{8,9},{9,8},{10,11... | collective-permute-start | bytes 5898248 | tf_op jit(solution)/shard_map/ppermute | solution.py:714
  726.1 23.9 %collective-permute-start.8 = (bf16[960,1024]{1,0:T(8,128)(2,1)}, bf16[960,1024]{1,0:T(8,128)(2,1)}, u32[]{:S(2)}, u32[]{:S(2)}) collective-permute-start(bf16[960,1024]{1,0:T(8,128)(2,1)} %collective-permute-done.refs_5_), channel_id=1, source_target_pairs={{0,1},{1,0},{2,3},{3,2},{4,5},{5,4},{6,7},{7,6},{8,9},{9,8},{10,11... | collective-permute-start | bytes 5898248 | tf_op jit(solution)/shard_map/ppermute | solution.py:714
  726.1 23.9 %collective-permute-start.9 = (bf16[960,1024]{1,0:T(8,128)(2,1)}, bf16[960,1024]{1,0:T(8,128)(2,1)}, u32[]{:S(2)}, u32[]{:S(2)}) collective-permute-start(bf16[960,1024]{1,0:T(8,128)(2,1)} %collective-permute-done.1.refs_8_), channel_id=1, source_target_pairs={{0,1},{1,0},{2,3},{3,2},{4,5},{5,4},{6,7},{7,6},{8,9},{9,8},{10,11... | collective-permute-start | bytes 5898248 | tf_op jit(solution)/shard_map/ppermute | solution.py:714
  726.6 45.1 %collective-permute-start.12 = (bf16[960,1024]{1,0:T(8,128)(2,1)}, bf16[960,1024]{1,0:T(8,128)(2,1)}, u32[]{:S(2)}, u32[]{:S(2)}) collective-permute-start(bf16[960,1024]{1,0:T(8,128)(2,1)} %collective-permute-done.1.refs_8_), channel_id=1, source_target_pairs={{0,2},{1,3},{2,0},{3,1},{4,6},{5,7},{6,4},{7,5},{8,10},{9,11},{10,... | collective-permute-start | bytes 5898248 | tf_op jit(solution)/shard_map/ppermute | solution.py:714
  729.9 45.2 %collective-permute-start.2 = (bf16[960,1024]{1,0:T(8,128)(2,1)}, bf16[960,1024]{1,0:T(8,128)(2,1)}, u32[]{:S(2)}, u32[]{:S(2)}) collective-permute-start(bf16[960,1024]{1,0:T(8,128)(2,1)} %collective-permute-done.refs_5_), channel_id=1, source_target_pairs={{0,4},{1,5},{2,6},{3,7},{4,0},{5,1},{6,2},{7,3},{8,12},{9,13},{10,... | collective-permute-start | bytes 5898248 | tf_op jit(solution)/shard_map/ppermute | solution.py:714
  771.7 7.0 collective-permute-start.13
  775.1 6.5 collective-permute-start.11
